TPU v7x, 16 devices: a 4x2x1 block of a 4x4x8 slice. The times are simulated.
16 devices in a mesh: dp: 2 (over y, z), sp: 8 (over x, core).
Axes of the slice: x: 4, y: 2, z: 1, core: 2. Of those that a mesh axis runs over, the one named last changes fastest.
The devices are a block of a 4x4x8 slice.
Arguments:
- pair_rep: float32 [384, 192, 128], P(('dp', 'sp')), parts along dimension 0
- w_qkvg_s: bfloat16 [128, 512], replicated
- w_bias_s: bfloat16 [4, 128], replicated
- w_out_s: bfloat16 [128, 128], replicated
- w_qkvg_e: bfloat16 [128, 512], replicated
- w_bias_e: bfloat16 [4, 128], replicated
- w_out_e: bfloat16 [128, 128], replicated
- w_one: bfloat16 [128, 512], replicated
- w_two: bfloat16 [512, 128], replicated
Outputs:
- output: float32 [384, 192, 128], P(('dp', 'sp')), parts along dimension 0
There are 2 independent parts. A program takes and returns all parts, laid end to end along the dimension named above; an argument that names none is the same for every part.
All inputs are finite; a program needn't handle non-finite values.
Results may differ from a plain program's by a relative error of at most 0.0102778.
Values are sent between devices in bfloat16 or wider.
A program may use at most 768 MiB of HBM per device.

v0:
```python
import jax
import jax.numpy as jnp
from jax import lax
from jax.sharding import PartitionSpec as P

LN_EPS = 1e-5
SCORE_CAP = 2 ** 23


def layer_norm(values):
    vals_f = values.astype(jnp.float32)
    mean_c = jnp.mean(vals_f, axis=-1, keepdims=True)
    centered = vals_f - mean_c
    variance = jnp.mean(centered * centered, axis=-1, keepdims=True)
    return (centered * lax.rsqrt(variance + LN_EPS)).astype(jnp.bfloat16)


def project(normed, w_qkvg, num_heads):
    channels = w_qkvg.shape[0]
    projected = jnp.dot(normed, w_qkvg, preferred_element_type=jnp.float32)
    split_shape = normed.shape[:-1] + (num_heads, channels // num_heads)
    queries = projected[..., :channels].astype(jnp.bfloat16).reshape(split_shape)
    key_vecs = projected[..., channels:2 * channels].astype(jnp.bfloat16).reshape(split_shape)
    val_vecs = projected[..., 2 * channels:3 * channels].astype(jnp.bfloat16).reshape(split_shape)
    gate_vals = jax.nn.sigmoid(projected[..., 3 * channels:]).reshape(split_shape)
    return queries, key_vecs, val_vecs, gate_vals


def attend(queries, key_vecs, val_vecs, gate_vals, bias_full, w_out, score_form, mix_form):
    head_dim = queries.shape[-1]
    scores = jnp.einsum(score_form, queries, key_vecs, preferred_element_type=jnp.float32)
    scores = scores * head_dim ** -0.5 + bias_full.astype(jnp.float32)
    attn_prob = jax.nn.softmax(scores, axis=-1).astype(jnp.bfloat16)
    attn_out = jnp.einsum(mix_form, attn_prob, val_vecs, preferred_element_type=jnp.float32)
    gated_out = (attn_out * gate_vals).astype(jnp.bfloat16)
    merged = gated_out.reshape(gated_out.shape[:-2] + (w_out.shape[0],))
    return jnp.dot(merged, w_out, preferred_element_type=jnp.float32)


def transition(resid_in, w_one, w_two):
    hidden = jax.nn.relu(jnp.dot(layer_norm(resid_in), w_one, preferred_element_type=jnp.float32))
    return jnp.dot(hidden.astype(jnp.bfloat16), w_two, preferred_element_type=jnp.float32)


def block_size(total_len, per_item):
    return max(candidate for candidate in range(1, total_len + 1) if total_len % candidate == 0 and (candidate == 1 or candidate * per_item <= SCORE_CAP))


def solution(mesh):
    row_spec = P(('dp', 'sp'), None, None)

    def local_fn(pair_loc, w_qkvg_s, w_bias_s, w_out_s, w_qkvg_e, w_bias_e, w_out_e, w_one, w_two):
        num_rows, seq_len, channels = pair_loc.shape
        num_heads = w_bias_s.shape[0]
        blk_rows = block_size(num_rows, num_heads * seq_len * seq_len)
        normed = layer_norm(pair_loc)
        bias_loc = jnp.einsum('hc,jkc->hjk', w_bias_s, normed, preferred_element_type=jnp.float32).astype(jnp.bfloat16)
        bias_s = lax.all_gather(bias_loc, 'sp', axis=1, tiled=True)

        def start_block(block_idx):
            normed_blk = lax.dynamic_slice_in_dim(normed, block_idx * blk_rows, blk_rows, axis=0)
            queries, key_vecs, val_vecs, gate_vals = project(normed_blk, w_qkvg_s, num_heads)
            return attend(queries, key_vecs, val_vecs, gate_vals, bias_s, w_out_s, 'rjhd,rkhd->rhjk', 'rhjk,rkhd->rjhd')

        start_upd = lax.map(start_block, jnp.arange(num_rows // blk_rows))
        pair_one = pair_loc + start_upd.reshape(num_rows, seq_len, channels)
        col_major = lax.all_to_all(pair_one.astype(jnp.bfloat16), 'sp', 1, 0, tiled=True)
        normed_c = layer_norm(col_major)
        bias_loc_e = jnp.einsum('hc,kic->hik', w_bias_e, normed_c, preferred_element_type=jnp.float32).astype(jnp.bfloat16)
        bias_e = lax.all_gather(bias_loc_e, 'sp', axis=1, tiled=True)

        def end_block(block_idx):
            normed_blk = lax.dynamic_slice_in_dim(normed_c, block_idx * blk_rows, blk_rows, axis=1)
            pair_blk = lax.dynamic_slice_in_dim(col_major, block_idx * blk_rows, blk_rows, axis=1)
            queries, key_vecs, val_vecs, gate_vals = project(normed_blk, w_qkvg_e, num_heads)
            end_upd = attend(queries, key_vecs, val_vecs, gate_vals, bias_e, w_out_e, 'ijhd,kjhd->jhik', 'jhik,kjhd->ijhd')
            pair_two = pair_blk.astype(jnp.float32) + end_upd
            return (end_upd + transition(pair_two, w_one, w_two)).astype(jnp.bfloat16)

        delta_blocks = lax.map(end_block, jnp.arange(num_rows // blk_rows))
        delta_cols = jnp.moveaxis(delta_blocks, 0, 1).reshape(seq_len, num_rows, channels)
        delta_rows = lax.all_to_all(delta_cols, 'sp', 0, 1, tiled=True)
        return pair_one + delta_rows.astype(jnp.float32)

    return jax.shard_map(local_fn, mesh=mesh, in_specs=(row_spec, P(), P(), P(), P(), P(), P(), P(), P()), out_specs=row_spec, check_vma=False)
```

profile of v0, /device:TPU:112, one launch (start us, length us, event | category | flops | bytes accessed | tf_op | source)
XLA Modules:
  0.0 210.9 jit_solution(12737751722046943576)
XLA Ops:
  0.0 2.7 %reduce_sum.76 = f32[24,192]{1,0:T(8,128)S(1)} reduce(f32[24,192,128]{2,1,0:T(8,128)} %param.9, f32[]{:T(128)} %constant.38.clone.1), dimensions={2}, to_apply=%region_0.0 | reduce | flops 585216 | bytes 2377732 | tf_op jit(solution)/shard_map/reduce_sum | solution.py:12
  2.7 1.7 multiply_reduce_fusion.1
  4.5 2.0 fusion.33
  6.5 24.7 %all_gather.6 = bf16[4,192,192]{2,0,1:T(4,128)(2,1)S(1)} all-gather(bf16[4,24,192]{2,0,1:T(4,128)(2,1)S(1)} %fusion.33), channel_id=1, replica_groups=mesh['dp'=2,'sp'=8] {'sp'}, dimensions={1}, use_global_device_ids=true | all-gather | bytes 331776 | tf_op jit(solution)/shard_map/all_gather | solution.py:58
  31.2 0.1 copy_convert_fusion.1
  31.3 1.2 copy.68
  32.5 4.7 %fusion.52 = (bf16[24,192,512]{2,1,0:T(8,128)(2,1)S(1)}, f32[24,192,512]{2,1,0:T(8,128)}) fusion(bf16[128,512]{1,0:T(8,128)(2,1)S(1)} %copy-done, f32[24,192,128]{2,1,0:T(8,128)S(1)} %copy-done.2, f32[24,192]{1,0:T(8,128)S(1)} %add_rsqrt_fusion.2, f32[24,192]{1,0:T(8,128)S(1)} %broadcast_multiply_fusion.2), kind=kOutput, calls=%fused_computation.77 | convolution fusion | flops 608108544 | bytes 16683008 | tf_op jit(solution)/shard_map/while/body/eval_jaxpr/dot_general | solution.py:20
  37.2 2.3 %fusion.51 = (bf16[24,192,128]{2,1,0:T(8,128)(2,1)}, bf16[24,192,128]{2,1,0:T(8,128)(2,1)}, bf16[24,192,128]{2,1,0:T(8,128)(2,1)}) fusion(bf16[24,192,512]{2,1,0:T(8,128)(2,1)S(1)} %get-tuple-element.47), kind=kLoop, calls=%fused_computation.76 | loop fusion | bytes 7077888 | tf_op jit(solution)/shard_map/while/body/eval_jaxpr/slice | solution.py:23
  39.5 2.5 %copy.66 = bf16[24,192,128]{1,2,0:T(8,128)(2,1)} copy(bf16[24,192,128]{2,1,0:T(8,128)(2,1)} %get-tuple-element.44) | data formatting | bytes 2359296 | tf_op jit(solution)/shard_map/while/body/eval_jaxpr/slice | solution.py:23
  42.0 2.5 %copy.65 = bf16[24,192,128]{1,2,0:T(8,128)(2,1)} copy(bf16[24,192,128]{2,1,0:T(8,128)(2,1)} %get-tuple-element.45) | data formatting | bytes 2359296 | tf_op jit(solution)/shard_map/while/body/eval_jaxpr/slice | solution.py:22
  44.5 2.6 %copy.64 = bf16[24,192,128]{1,2,0:T(8,128)(2,1)} copy(bf16[24,192,128]{2,1,0:T(8,128)(2,1)} %get-tuple-element.46) | data formatting | bytes 2359296 | tf_op jit(solution)/shard_map/while/body/eval_jaxpr/slice | solution.py:24
  47.1 3.7 %fusion.25 = f32[24,192,128]{2,1,0:T(8,128)} fusion(f32[24,192,512]{2,1,0:T(8,128)} %get-tuple-element.48), kind=kLoop, calls=%fused_computation.33 | loop fusion | flops 1769472 | bytes 4718592 | tf_op jit(solution)/shard_map/while/body/eval_jaxpr/div | solution.py:25
  50.8 3.5 %copy.70 = f32[24,192,128]{1,2,0:T(8,128)} copy(f32[24,192,128]{2,1,0:T(8,128)} %fusion.25) | data formatting | bytes 4718592 | tf_op jit(solution)/shard_map/while/body/eval_jaxpr/div | solution.py:25
  54.3 11.8 %fusion.53 = (f32[24,4,192]{2,1,0:T(4,128)S(1)}, f32[24,4,192,192]{2,3,1,0:T(8,128)}) fusion(bf16[24,192,4,32]{1,3,2,0:T(8,128)(2,1)} %bitcast.97, bf16[24,192,4,32]{1,3,2,0:T(8,128)(2,1)} %bitcast.95, f32[4,192,192]{1,2,0:T(8,128)S(1)} %copy-done.6), kind=kOutput, calls=%fused_computation.78 | convolution fusion | flops 240648384 | bytes 17178624 | tf_op jit(solution)/shard_map/while/body/eval_jaxpr/sub | solution.py:33
  66.1 0.0 copy-start.9
  66.2 9.6 %fusion.19 = bf16[24,192,4,32]{1,3,2,0:T(8,128)(2,1)S(1)} fusion(f32[24,192,4,32]{1,3,2,0:T(8,128)} %bitcast.92, bf16[24,192,4,32]{1,3,2,0:T(8,128)(2,1)} %bitcast.98, f32[24,4,192,192]{2,3,1,0:T(8,128)} %get-tuple-element.50, f32[24,4,192]{2,1,0:T(4,128)S(1)} %get-tuple-element.49), kind=kOutput, calls=%fused_computation.25 | convolution fusion | flops 234749952 | bytes 18948096 | tf_op jit(solution)/shard_map/while/body/eval_jaxpr/rhjk,rkhd->rjhd/dot_general | solution.py:34
  75.8 2.0 fusion.54
  77.8 0.8 copy.72
  78.6 19.9 %all_to_all.8 = bf16[24,192,128]{2,0,1:T(8,128)(2,1)S(1)} all-to-all(bf16[24,192,128]{2,0,1:T(8,128)(2,1)S(1)} %copy.72), channel_id=1, replica_groups=mesh['dp'=2,'sp'=8] {'sp'}, dimensions={1} | all-to-all | bytes 2359296 | tf_op jit(solution)/shard_map/all_to_all | solution.py:67
  98.5 0.2 convert.20
  98.6 0.2 copy.73
  98.8 0.0 copy-start.14
  98.8 0.7 bitcast_reduce_fusion
  99.5 1.4 fusion.27
  101.0 2.9 %fusion.32 = bf16[4,24,192]{1,0,2:T(4,128)(2,1)S(1)} fusion(f32[192,24,128]{2,1,0:T(8,128)S(1)} %bitcast.86, f32[192,24]{1,0:T(8,128)S(1)} %bitcast.104, f32[192,24]{1,0:T(8,128)S(1)} %bitcast.102, bf16[4,128]{1,0:T(4,128)(2,1)S(1)} %copy-done.14), kind=kOutput, calls=%fused_computation.49 | convolution fusion | flops 6506496 | bytes 2434048 | tf_op jit(solution)/shard_map/hc,kic->hik/dot_general | solution.py:69
  103.8 0.2 copy.77
  104.0 22.1 %all_gather.7 = bf16[4,192,192]{2,0,1:T(4,128)(2,1)S(1)} all-gather(bf16[4,24,192]{2,0,1:T(4,128)(2,1)S(1)} %copy.77), channel_id=1, replica_groups=mesh['dp'=2,'sp'=8] {'sp'}, dimensions={1}, use_global_device_ids=true | all-gather | bytes 331776 | tf_op jit(solution)/shard_map/all_gather | solution.py:70
  126.1 0.1 copy_convert_fusion
  126.2 1.2 copy.79
  127.4 4.7 %fusion.55 = (bf16[192,24,512]{2,1,0:T(8,128)(2,1)S(1)}, f32[192,24,512]{2,1,0:T(8,128)}) fusion(bf16[128,512]{1,0:T(8,128)(2,1)S(1)} %copy-done.8, f32[192,24,128]{2,1,0:T(8,128)S(1)} %bitcast.87, f32[192,24]{1,0:T(8,128)S(1)} %bitcast.105, f32[192,24]{1,0:T(8,128)S(1)} %bitcast.103), kind=kOutput, calls=%fused_computation.80 | convolution fusion | flops 608108544 | bytes 16683008 | tf_op jit(solution)/shard_map/while/body/eval_jaxpr/dot_general | solution.py:20
  132.1 2.0 fusion.50
  134.1 2.9 %copy.76 = bf16[192,24,128]{0,2,1:T(8,128)(2,1)} copy(bf16[192,24,128]{2,1,0:T(8,128)(2,1)} %get-tuple-element.32) | data formatting | bytes 2359296 | tf_op jit(solution)/shard_map/while/body/eval_jaxpr/slice | solution.py:23
  137.1 2.8 %copy.75 = bf16[192,24,128]{0,2,1:T(8,128)(2,1)} copy(bf16[192,24,128]{2,1,0:T(8,128)(2,1)} %get-tuple-element.42) | data formatting | bytes 2359296 | tf_op jit(solution)/shard_map/while/body/eval_jaxpr/slice | solution.py:22
  139.9 2.9 %copy.74 = bf16[192,24,128]{0,2,1:T(8,128)(2,1)} copy(bf16[192,24,128]{2,1,0:T(8,128)(2,1)} %get-tuple-element.43) | data formatting | bytes 2359296 | tf_op jit(solution)/shard_map/while/body/eval_jaxpr/slice | solution.py:24
  142.8 3.7 %fusion.22 = f32[192,24,128]{2,1,0:T(8,128)} fusion(f32[192,24,512]{2,1,0:T(8,128)} %get-tuple-element.65), kind=kLoop, calls=%fused_computation.29 | loop fusion | flops 1769472 | bytes 4718592 | tf_op jit(solution)/shard_map/while/body/eval_jaxpr/div | solution.py:25
  146.4 3.7 %copy.81 = f32[192,24,128]{0,2,1:T(8,128)} copy(f32[192,24,128]{2,1,0:T(8,128)} %fusion.22) | data formatting | bytes 4718592 | tf_op jit(solution)/shard_map/while/body/eval_jaxpr/div | solution.py:25
  150.1 11.8 %fusion.56 = (f32[24,4,192]{2,1,0:T(4,128)S(1)}, f32[24,4,192,192]{2,3,1,0:T(8,128)}) fusion(bf16[192,24,4,32]{0,3,2,1:T(8,128)(2,1)} %bitcast.99, bf16[192,24,4,32]{0,3,2,1:T(8,128)(2,1)} %bitcast.96, f32[4,192,192]{1,2,0:T(8,128)S(1)} %copy-done.7), kind=kOutput, calls=%fused_computation.81 | convolution fusion | flops 240648384 | bytes 17178624 | tf_op jit(solution)/shard_map/while/body/eval_jaxpr/sub | solution.py:33
  162.0 10.8 %fusion.18 = bf16[192,24,4,32]{0,3,2,1:T(8,128)(2,1)} fusion(f32[192,24,4,32]{0,3,2,1:T(8,128)} %bitcast.93, bf16[192,24,4,32]{0,3,2,1:T(8,128)(2,1)} %bitcast.100, f32[24,4,192,192]{2,3,1,0:T(8,128)} %get-tuple-element.67, f32[24,4,192]{2,1,0:T(4,128)S(1)} %get-tuple-element.66), kind=kOutput, calls=%fused_computation.23 | convolution fusion | flops 234749952 | bytes 18948096 | tf_op jit(solution)/shard_map/while/body/eval_jaxpr/jhik,kjhd->ijhd/dot_general | solution.py:34
  172.7 2.6 %copy.82 = bf16[192,24,128]{2,1,0:T(8,128)(2,1)} copy(bf16[192,24,128]{0,2,1:T(8,128)(2,1)} %bitcast.101) | data formatting | bytes 2359296 | tf_op jit(solution)/shard_map/while/body/eval_jaxpr/reshape | solution.py:36
  175.4 3.4 %fusion.49 = (f32[192,24]{1,0:T(8,128)S(1)}, f32[192,24,128]{2,1,0:T(8,128)S(1)}, f32[192,24,128]{2,1,0:T(8,128)}) fusion(f32[192,24,128]{2,1,0:T(8,128)S(1)} %bitcast.88, bf16[192,24,128]{2,1,0:T(8,128)(2,1)} %copy.82, bf16[128,128]{1,0:T(8,128)(2,1)S(1)} %copy-done.10), kind=kOutput, calls=%fused_computation.74 | convolution fusion | flops 152169984 | bytes 8308736 | tf_op jit(solution)/shard_map/while/body/eval_jaxpr/dot_general | solution.py:37
  178.8 1.4 copy-done.4
  180.2 1.4 multiply_reduce_fusion
  181.7 5.2 %add_convert_fusion = bf16[192,24,128]{2,1,0:T(8,128)(2,1)} fusion(f32[192,24,128]{2,1,0:T(8,128)S(1)} %copy-done.5, f32[192,24,128]{2,1,0:T(8,128)} %copy-done.4, f32[192,24]{1,0:T(8,128)S(1)} %add_rsqrt_fusion, f32[192,24]{1,0:T(8,128)S(1)} %broadcast_multiply_fusion, bf16[512,128]{1,0:T(8,128)(2,1)S(1)} %copy-done.12, bf16[128,512]{1,0:T(8,128)(2,1)S(1)} %copy-done.13), kind=kOutput, calls=%fused_computation.39 | convolution fusion | flops 1215627264 | bytes 6197248 | tf_op jit(solution)/shard_map/while/body/eval_jaxpr/dot_general | solution.py:42
  186.9 20.7 %all_to_all.9 = bf16[192,24,128]{2,1,0:T(8,128)(2,1)S(1)} all-to-all(bf16[192,24,128]{2,1,0:T(8,128)(2,1)} %add_convert_fusion), channel_id=1, replica_groups=mesh['dp'=2,'sp'=8] {'sp'}, dimensions={0} | all-to-all | bytes 2359296 | tf_op jit(solution)/shard_map/all_to_all | solution.py:82
  207.6 0.3 copy.83
  207.8 0.0 copy-start.1
  207.8 1.4 copy-done.3
  209.2 1.7 bitcast_add_fusion
  (31 shorter events, 0.1 us)
Async XLA Ops:
  0.0 32.5 %copy-start = (bf16[128,512]{1,0:T(8,128)(2,1)S(1)}, bf16[128,512]{1,0:T(8,128)(2,1)}, u32[]{:S(2)}) copy-start(bf16[128,512]{1,0:T(8,128)(2,1)} %param.10) | copy-start | bytes 393220
  0.0 2.7 %copy-start.2 = (f32[24,192,128]{2,1,0:T(8,128)S(1)}, f32[24,192,128]{2,1,0:T(8,128)}, u32[]{:S(2)}) copy-start(f32[24,192,128]{2,1,0:T(8,128)} %param.9) | copy-start | bytes 7077892
  0.0 4.5 %copy-start.11 = (bf16[4,128]{1,0:T(4,128)(2,1)S(1)}, bf16[4,128]{1,0:T(4,128)(2,1)}, u32[]{:S(2)}) copy-start(bf16[4,128]{1,0:T(4,128)(2,1)} %param.11) | copy-start | bytes 3076
  50.8 3.5 %copy-start.6 = (f32[4,192,192]{1,2,0:T(8,128)S(1)}, f32[4,192,192]{1,2,0:T(8,128)}, u32[]{:S(2)}) copy-start(f32[4,192,192]{1,2,0:T(8,128)} %copy.68) | copy-start | bytes 1769476
  66.1 9.6 %copy-start.9 = (bf16[128,128]{1,0:T(8,128)(2,1)S(1)}, bf16[128,128]{1,0:T(8,128)(2,1)}, u32[]{:S(2)}) copy-start(bf16[128,128]{1,0:T(8,128)(2,1)} %param.12) | copy-start | bytes 98308
  98.8 2.2 %copy-start.14 = (bf16[4,128]{1,0:T(4,128)(2,1)S(1)}, bf16[4,128]{1,0:T(4,128)(2,1)}, u32[]{:S(2)}) copy-start(bf16[4,128]{1,0:T(4,128)(2,1)} %param.14) | copy-start | bytes 3076
  103.8 23.6 %copy-start.8 = (bf16[128,512]{1,0:T(8,128)(2,1)S(1)}, bf16[128,512]{1,0:T(8,128)(2,1)}, u32[]{:S(2)}) copy-start(bf16[128,512]{1,0:T(8,128)(2,1)} %param.13) | copy-start | bytes 393220
  146.4 3.7 %copy-start.7 = (f32[4,192,192]{1,2,0:T(8,128)S(1)}, f32[4,192,192]{1,2,0:T(8,128)}, u32[]{:S(2)}) copy-start(f32[4,192,192]{1,2,0:T(8,128)} %copy.79) | copy-start | bytes 1769476
  172.7 2.6 %copy-start.10 = (bf16[128,128]{1,0:T(8,128)(2,1)S(1)}, bf16[128,128]{1,0:T(8,128)(2,1)}, u32[]{:S(2)}) copy-start(bf16[128,128]{1,0:T(8,128)(2,1)} %param.15) | copy-start | bytes 98308
  178.8 1.4 copy-start.4
  178.8 2.9 %copy-start.5 = (f32[192,24,128]{2,1,0:T(8,128)S(1)}, f32[192,24,128]{2,1,0:T(8,128)}, u32[]{:S(2)}) copy-start(f32[192,24,128]{2,1,0:T(8,128)} %get-tuple-element.68) | copy-start | bytes 7077892
  178.8 2.9 %copy-start.12 = (bf16[512,128]{1,0:T(8,128)(2,1)S(1)}, bf16[512,128]{1,0:T(8,128)(2,1)}, u32[]{:S(2)}) copy-start(bf16[512,128]{1,0:T(8,128)(2,1)} %param.17) | copy-start | bytes 393220
  178.8 2.9 %copy-start.13 = (bf16[128,512]{1,0:T(8,128)(2,1)S(1)}, bf16[128,512]{1,0:T(8,128)(2,1)}, u32[]{:S(2)}) copy-start(bf16[128,512]{1,0:T(8,128)(2,1)} %param.16) | copy-start | bytes 393220
  207.6 1.7 copy-start.3
  207.8 3.1 %copy-start.1 = (bf16[128,512]{1,0:T(8,128)(2,1)S(1)}, bf16[128,512]{1,0:T(8,128)(2,1)}, u32[]{:S(2)}) copy-start(bf16[128,512]{1,0:T(8,128)(2,1)} %param.10) | copy-start | bytes 393220
where the time goes:
time: 211 us
  blocking collectives  87.4 us (41%)
  matrix products  69 us (33%)
  local copies, waits for them, and re-layouts  36.9 us (17%)
  other arithmetic  17.3 us (8%)
    all_gather x1, blocking collectives, local_fn(): bias_s = lax.all_gather(bias_loc, 'sp', axis=1, tiled=True)  24.7 us
    sub x2, matrix products, attend(): attn_prob = jax.nn.softmax(scores, axis=-1).astype(jnp.bfloat16)  23.7 us
    all_gather x1, blocking collectives, local_fn(): bias_e = lax.all_gather(bias_loc_e, 'sp', axis=1, tiled=True)  22.1 us
    all_to_all x1, blocking collectives, local_fn(): delta_rows = lax.all_to_all(delta_cols, 'sp', 0, 1, tiled=True)  20.7 us
    dot_general x2, matrix products, attend(): jnp.einsum(mix_form, attn_prob, val_vecs, preferred_element_type=jnp.floa...  20.4 us
    all_to_all x1, blocking collectives, local_fn(): lax.all_to_all(pair_one.astype(jnp.bfloat16), 'sp', 1, 0, tiled=True)  19.9 us
    slice x4, local copies, waits for them, and re-layouts, project(): projected[..., channels:2 * channels].astype(jnp.bfloat16)  9.71 us
    dot_general x2, matrix products, project(): projected = jnp.dot(normed, w_qkvg, preferred_element_type=jnp.float32)  9.44 us

commit v1 on v0

v1 whole, which is shorter than its diff:
```python
import functools

import jax
import jax.numpy as jnp
from jax import lax
from jax.experimental import pallas as pl
from jax.experimental.pallas import tpu as pltpu
from jax.sharding import PartitionSpec as P

LN_EPS = 1e-5
MESH = pl.DeviceIdType.MESH
F32 = jnp.float32
BF16 = jnp.bfloat16


def layer_norm(vals):
    mean_c = jnp.mean(vals, axis=-1, keepdims=True)
    centered = vals - mean_c
    variance = jnp.mean(centered * centered, axis=-1, keepdims=True)
    return (centered * lax.rsqrt(variance + LN_EPS)).astype(BF16)


def dot(lhs, rhs, lhs_dim=1, rhs_dim=0):
    return lax.dot_general(lhs, rhs, (((lhs_dim,), (rhs_dim,)), ((), ())), preferred_element_type=F32)


def duplicate_tail(normed):
    return jnp.concatenate([normed, normed[128:]], axis=0)


def low_half(shape):
    return lax.broadcasted_iota(jnp.int32, shape, len(shape) - 1) < 64


def bias_row(normed_dup, w_bias):
    full = dot(w_bias, normed_dup, 1, 1)
    low = low_half((1, 128))
    tiles = []
    for first in (0, 2):
        head_a, head_b = full[first:first + 1], full[first + 1:first + 2]
        tiles += [head_a[:, :128], jnp.where(low, head_a[:, 128:], head_b[:, 128:]), head_b[:, :128]]
    return jnp.concatenate(tiles, axis=1)


def project(normed_dup, w_t, w_key):
    cols = dot(w_t, normed_dup, 1, 1)
    channels = w_key.shape[0]
    q_t = cols[:channels].astype(BF16)
    v_t = cols[channels:2 * channels, :192].astype(BF16)
    g_t = jax.nn.sigmoid(cols[2 * channels:])
    keys = dot(normed_dup[:192], w_key).astype(BF16)
    return q_t, keys, v_t, g_t


def attend(q_t, keys, v_t, g_t, bias_of, w_out, scale):
    zero = jnp.zeros((32, 128), BF16)
    low = low_half((32, 128))

    def head(idx):
        return q_t[32 * idx:32 * idx + 32, :128], q_t[32 * idx:32 * idx + 32, 128:]

    q0, q0b = head(0)
    q1, q1b = head(1)
    q2, q2b = head(2)
    q3, q3b = head(3)

    def lo(val):
        return jnp.where(low, val, jnp.zeros_like(val))

    def hi(val):
        return jnp.where(low, jnp.zeros_like(val), val)

    def stack(rows):
        return jnp.concatenate([jnp.concatenate(row, axis=1) for row in rows], axis=0)

    none = [zero, zero]
    blocks = [
        stack([[q0, lo(q0b)], [zero, hi(q1b)], none, none]),
        stack([none, [q1, zero], [zero, q2], none]),
        stack([none, none, [lo(q2b), zero], [hi(q3b), q3]]),
    ]
    outs = []
    for tile, block in enumerate(blocks):
        scores = dot(keys, block) * scale + bias_of(tile)
        top = jnp.max(scores, axis=0, keepdims=True)
        prob = jnp.exp(scores - top)
        total = jnp.sum(prob, axis=0, keepdims=True)
        mixed = dot(v_t[32 * tile:32 * tile + 64], prob.astype(BF16))
        outs.append(mixed / total)
    main = jnp.concatenate([outs[0][:32, :128], outs[1][:32, :128], outs[1][32:, 128:], outs[2][32:, 128:]], axis=0)
    tail = jnp.concatenate([lo(outs[0][:32, 128:]), hi(outs[0][32:, 128:]), lo(outs[2][:32, :128]), hi(outs[2][32:, :128])], axis=0)
    gated = (jnp.concatenate([main, tail], axis=1) * g_t).astype(BF16)
    res = dot(gated.T, w_out)
    return jnp.concatenate([res[:128], res[128:192] + res[192:]], axis=0)


def kernel(axis, group, z_ref, wp_s, wb_s, wo_s, wp_e, wb_e, wo_e, w1_ref, w2_ref, y_ref,
           wt_s, wt_e, row_bias, send_bias, got_bias, bias_t, q_sc, k_sc, v_sc, g_sc,
           send_h, got_h, send_d, got_d, flat,
           bias_send_sem, bias_recv_sem, h_send_sem, h_recv_sem, d_send_sem, d_recv_sem):
    rows, seq_len, channels = z_ref.shape
    pairs = rows // 2
    scale = 32 ** -0.5
    me = lax.axis_index(axis)
    peers = [lax.rem(me + step, group) for step in range(1, group)]

    barrier = pltpu.get_barrier_semaphore()
    for peer in peers:
        pl.semaphore_signal(barrier, inc=1, device_id={axis: peer}, device_id_type=MESH)

    for wp, wt in ((wp_s, wt_s), (wp_e, wt_e)):
        wt[0:channels] = wp[:, 0:channels].T
        wt[channels:2 * channels] = wp[:, 2 * channels:3 * channels].T
        wt[2 * channels:3 * channels] = wp[:, 3 * channels:].T

    def copy_bias(phase, peer):
        return pltpu.make_async_remote_copy(
            src_ref=send_bias.at[phase], dst_ref=got_bias.at[phase, me],
            send_sem=bias_send_sem.at[phase, peer], recv_sem=bias_recv_sem.at[phase, me],
            device_id={axis: peer}, device_id_type=MESH)

    def wait_bias(phase):
        for peer in peers:
            pltpu.make_async_copy(got_bias.at[phase, peer], got_bias.at[phase, peer], bias_recv_sem.at[phase, peer]).wait()

    def copy_pair(send, got, send_sem, recv_sem, peer, pair):
        return pltpu.make_async_remote_copy(
            src_ref=send.at[peer, pair], dst_ref=got.at[me, pair],
            send_sem=send_sem.at[peer], recv_sem=recv_sem.at[me],
            device_id={axis: peer}, device_id_type=MESH)

    def wait_all(got, recv_sem):
        for peer in peers:
            pltpu.make_async_copy(got.at[peer], got.at[peer], recv_sem.at[peer]).wait()

    def store_pair(send, got, pair, first, second):
        for dest in range(group):
            span = slice(rows * dest, rows * dest + rows)
            send[dest, pair] = jnp.concatenate([first[span], second[span]], axis=0).astype(BF16)
        got[me, pair] = send[me, pair]

    def publish_bias(phase):
        rounded = row_bias[...].astype(BF16)
        send_bias[phase] = rounded
        got_bias[phase, me] = rounded

    def stage_projection(slot, normed_dup, wt, wp):
        q_t, keys, v_t, g_t = project(normed_dup, wt[...], wp[:, channels:2 * channels])
        q_sc[slot] = q_t
        k_sc[slot] = keys
        v_sc[slot] = v_t
        g_sc[slot] = g_t

    def staged_attention(slot, wo):
        return attend(q_sc[slot], k_sc[slot], v_sc[slot], g_sc[slot],
                      lambda tile: bias_t[:, 256 * tile:256 * tile + 256], wo[...], scale)

    @pl.loop(0, rows)
    def _(row):
        normed_dup = duplicate_tail(layer_norm(z_ref[row]))
        row_bias[pl.ds(row, 1), :] = bias_row(normed_dup, wb_s[...])

    publish_bias(0)
    pl.semaphore_wait(barrier, group - 1)
    for peer in peers:
        copy_bias(0, peer).start()

    @pl.loop(0, rows)
    def _(row):
        normed_dup = duplicate_tail(layer_norm(z_ref[row]))
        stage_projection(row, normed_dup, wt_s, wp_s)

    wait_bias(0)
    low = low_half((64, 128))
    by_query = jnp.concatenate([got_bias[0, src].astype(F32) for src in range(group)], axis=0)
    by_query = jnp.concatenate([by_query, by_query[128:]], axis=0)
    for first in (0, 1):
        base = 384 * first
        head_a = by_query[:, base:base + 128].T
        mixed = by_query[:, base + 128:base + 256].T
        head_b = by_query[:, base + 256:base + 384].T
        bias_t[0:128, base:base + 128] = head_a[:, :128]
        bias_t[128:192, base:base + 128] = mixed[:64, :128]
        low_a = low_half((128, 128))
        bias_t[0:128, base + 128:base + 256] = jnp.where(low_a, head_a[:, 128:], head_b[:, 128:])
        bias_t[128:192, base + 128:base + 256] = jnp.where(low, mixed[:64, 128:], mixed[64:, 128:])
        bias_t[0:128, base + 256:base + 384] = head_b[:, :128]
        bias_t[128:192, base + 256:base + 384] = mixed[64:, :128]

    @pl.loop(0, pairs)
    def _(pair):
        resid = []
        for sub in range(2):
            row = 2 * pair + sub
            value = z_ref[row] + staged_attention(row, wo_s)
            y_ref[row] = value
            resid.append(value)
            again = value.astype(BF16).astype(F32)
            row_bias[pl.ds(row, 1), :] = bias_row(duplicate_tail(layer_norm(again)), wb_e[...])
        store_pair(send_h, got_h, pair, resid[0], resid[1])

        @pl.when(pair > 0)
        def _():
            for peer in peers:
                copy_pair(send_h, got_h, h_send_sem, h_recv_sem, peer, pair - 1).start()

    publish_bias(1)
    for peer in peers:
        copy_pair(send_h, got_h, h_send_sem, h_recv_sem, peer, pairs - 1).start()
    for peer in peers:
        copy_bias(1, peer).start()

    wait_all(got_h, h_recv_sem)

    @pl.loop(0, group)
    def _(src):
        @pl.loop(0, pairs)
        def _(pair):
            start = pl.multiple_of((src * pairs + pair) * 2 * rows, 2 * rows)
            flat[pl.ds(start, 2 * rows), :] = got_h[src, pair].astype(F32)

    wait_bias(1)
    for src in range(group):
        bias_t[rows * src:rows * src + rows] = got_bias[1, src].astype(F32)

    @pl.loop(0, pairs)
    def _(pair):
        delta = []
        for sub in range(2):
            col = 2 * pair + sub
            trans = flat[pl.ds(col, seq_len, stride=rows), :]
            stage_projection(sub, duplicate_tail(layer_norm(trans)), wt_e, wp_e)
            upd = staged_attention(sub, wo_e)
            hidden = jnp.maximum(dot(layer_norm(trans + upd), w1_ref[...]), 0.0).astype(BF16)
            delta.append(upd + dot(hidden, w2_ref[...]))
        store_pair(send_d, got_d, pair, delta[0], delta[1])

        @pl.when(pair > 0)
        def _():
            for peer in peers:
                copy_pair(send_d, got_d, d_send_sem, d_recv_sem, peer, pair - 1).start()

    for peer in peers:
        copy_pair(send_d, got_d, d_send_sem, d_recv_sem, peer, pairs - 1).start()

    wait_all(got_d, d_recv_sem)

    @pl.loop(0, group)
    def _(src):
        @pl.loop(0, pairs)
        def _(pair):
            start = pl.multiple_of((src * pairs + pair) * 2 * rows, 2 * rows)
            flat[pl.ds(start, 2 * rows), :] = got_d[src, pair].astype(F32)

    @pl.loop(0, rows)
    def _(row):
        y_ref[row] = y_ref[row] + flat[pl.ds(row, seq_len, stride=rows), :]

    for peer in peers:
        for phase in range(2):
            pltpu.make_async_copy(send_bias.at[phase], send_bias.at[phase], bias_send_sem.at[phase, peer]).wait()
        pltpu.make_async_copy(send_h.at[peer], send_h.at[peer], h_send_sem.at[peer]).wait()
        pltpu.make_async_copy(send_d.at[peer], send_d.at[peer], d_send_sem.at[peer]).wait()


def solution(mesh):
    row_spec = P(('dp', 'sp'), None, None)
    group = mesh.shape['sp']

    def local_fn(pair_loc, w_qkvg_s, w_bias_s, w_out_s, w_qkvg_e, w_bias_e, w_out_e, w_one, w_two):
        rows, seq_len, channels = pair_loc.shape
        heads = w_bias_s.shape[0]
        pairs = rows // 2
        vmem = pl.BlockSpec(memory_space=pltpu.VMEM)
        wide = heads * seq_len
        exchange = pltpu.VMEM((group, pairs, 2 * rows, channels), BF16)
        return pl.pallas_call(
            functools.partial(kernel, 'sp', group),
            out_shape=jax.ShapeDtypeStruct(pair_loc.shape, F32),
            in_specs=[vmem] * 9,
            out_specs=vmem,
            scratch_shapes=[
                pltpu.VMEM((3 * channels, channels), BF16),
                pltpu.VMEM((3 * channels, channels), BF16),
                pltpu.VMEM((rows, wide), F32),
                pltpu.VMEM((2, rows, wide), BF16),
                pltpu.VMEM((2, group, rows, wide), BF16),
                pltpu.VMEM((seq_len, wide), F32),
                pltpu.VMEM((rows, channels, 256), BF16),
                pltpu.VMEM((rows, seq_len, channels), BF16),
                pltpu.VMEM((rows, channels, seq_len), BF16),
                pltpu.VMEM((rows, channels, 256), F32),
                exchange, exchange, exchange, exchange,
                pltpu.VMEM((rows * seq_len, channels), F32),
                pltpu.SemaphoreType.DMA((2, group)),
                pltpu.SemaphoreType.DMA((2, group)),
                pltpu.SemaphoreType.DMA((group,)),
                pltpu.SemaphoreType.DMA((group,)),
                pltpu.SemaphoreType.DMA((group,)),
                pltpu.SemaphoreType.DMA((group,)),
            ],
            compiler_params=pltpu.CompilerParams(collective_id=0, has_side_effects=True, vmem_limit_bytes=60 * 1024 * 1024),
        )(pair_loc, w_qkvg_s, w_bias_s, w_out_s, w_qkvg_e, w_bias_e, w_out_e, w_one, w_two)

    return jax.shard_map(local_fn, mesh=mesh, in_specs=(row_spec, P(), P(), P(), P(), P(), P(), P(), P()), out_specs=row_spec, check_vma=False)
```

time: 211 us -> 110 us (0.52)
  Pallas kernels: 0 us -> 106 us
  blocking collectives: 87.4 us -> 0 us
  matrix products: 69 us -> 0 us
  local copies, waits for them, and re-layouts: 36.9 us -> 3.3 us
  other arithmetic: 17.3 us -> 0 us
    pallas_call x0 -> x1, Pallas kernels: none -> 106 us  [local_fn(): pl.pallas_call(functools.partial(kernel, 'sp', group), out_shape=jax.Shap...]
    all_gather x2 -> x0, blocking collectives: 46.9 us -> none  [the longest x1 24.7 us: local_fn(): bias_s = lax.all_gather(bias_loc, 'sp', axis=1, tiled=True)]
    dot_general x9 -> x0, matrix products: 45.3 us -> none  [the longest x2 20.4 us: attend(): jnp.einsum(mix_form, attn_prob, val_vecs, preferred_element_type=jnp.floa...]
    all_to_all x2 -> x0, blocking collectives: 40.6 us -> none  [the longest x1 20.7 us: local_fn(): delta_rows = lax.all_to_all(delta_cols, 'sp', 0, 1, tiled=True)]
    sub x2 -> x0, matrix products: 23.7 us -> none  [attend(): attn_prob = jax.nn.softmax(scores, axis=-1).astype(jnp.bfloat16)]
    slice x8 -> x0, local copies, waits for them, and re-layouts: 20.5 us -> none  [the longest x4 9.71 us: project(): projected[..., channels:2 * channels].astype(jnp.bfloat16)]
    reduce_sum x5 -> x0, other arithmetic: 7.95 us -> none  [the longest x3 4.58 us: layer_norm(): variance = jnp.mean(centered * centered, axis=-1, keepdims=True)]
    div x5 -> x0, other arithmetic: 7.39 us -> none  [the longest x2 7.37 us: project(): jax.nn.sigmoid(projected[..., 3 * channels:]).reshape(split_shape)]
where the time goes in v1:
time: 110 us
  Pallas kernels  106 us (96%)
  local copies, waits for them, and re-layouts  3.3 us (3%)
    pallas_call x1, Pallas kernels, local_fn(): pl.pallas_call(functools.partial(kernel, 'sp', group), out_shape=jax.Shap...  106 us
    unnamed x1, local copies, waits for them, and re-layouts  3.3 us

profile of v1, /device:TPU:112, one launch (start us, length us, event | category | flops | bytes accessed | tf_op | source)
XLA Modules:
  0.0 109.7 jit_solution(13637946527167090042)
XLA Ops:
  0.0 106.4 %shard_map.91 = f32[24,192,128]{2,1,0:T(8,128)} custom-call(f32[24,192,128]{2,1,0:T(8,128)} %z_ref.1, bf16[128,512]{1,0:T(8,128)(2,1)} %wp_s.1, bf16[4,128]{1,0:T(4,128)(2,1)} %wb_s.1, bf16[128,128]{1,0:T(8,128)(2,1)} %wo_s.1, bf16[128,512]{1,0:T(8,128)(2,1)} %wp_e.1, bf16[4,128]{1,0:T(4,128)(2,1)} %wb_e.1, bf16[128,128]{1,0:T(8,128)(2,1)} %wo_e.1, ...), custom_call_target="tpu_custom_call" | custom-call | tf_op jit(solution)/shard_map/pallas_call | solution.py:277
  106.4 3.3 %copy.11 = f32[24,192,128]{2,1,0:T(8,128)} copy(f32[24,192,128]{2,1,0:T(8,128)} %shard_map.91) | data formatting | bytes 4718592

commit v2 on v1

v2 whole, which is shorter than its diff:
```python
import functools

import jax
import jax.numpy as jnp
from jax import lax
from jax.experimental import pallas as pl
from jax.experimental.pallas import tpu as pltpu
from jax.sharding import PartitionSpec as P

LN_EPS = 1e-5
MESH = pl.DeviceIdType.MESH
F32 = jnp.float32
BF16 = jnp.bfloat16


def layer_norm(vals):
    mean_c = jnp.mean(vals, axis=-1, keepdims=True)
    centered = vals - mean_c
    variance = jnp.mean(centered * centered, axis=-1, keepdims=True)
    return (centered * lax.rsqrt(variance + LN_EPS)).astype(BF16)


def dot(lhs, rhs, lhs_dim=1, rhs_dim=0):
    return lax.dot_general(lhs, rhs, (((lhs_dim,), (rhs_dim,)), ((), ())), preferred_element_type=F32)


def duplicate_tail(normed):
    return jnp.concatenate([normed, normed[128:]], axis=0)


def low_half(shape):
    return lax.broadcasted_iota(jnp.int32, shape, len(shape) - 1) < 64


def bias_row(full):
    low = low_half((1, 128))
    tiles = []
    for first in (0, 2):
        head_a, head_b = full[first:first + 1], full[first + 1:first + 2]
        tiles += [head_a[:, :128], jnp.where(low, head_a[:, 128:], head_b[:, 128:]), head_b[:, :128]]
    return jnp.concatenate(tiles, axis=1)


def keep_low(val):
    return jnp.where(low_half(val.shape), val, jnp.zeros_like(val))


def keep_high(val):
    return jnp.where(low_half(val.shape), jnp.zeros_like(val), val)


def stack(rows):
    return jnp.concatenate([jnp.concatenate(row, axis=1) for row in rows], axis=0)


def score_block(q_t, tile):
    zero = jnp.zeros((32, 128), BF16)
    none = [zero, zero]

    def head(idx):
        return q_t[32 * idx:32 * idx + 32, :128], q_t[32 * idx:32 * idx + 32, 128:]

    first, second = head(tile), head(tile + 1)
    if tile == 0:
        return stack([[first[0], keep_low(first[1])], [zero, keep_high(second[1])], none, none])
    if tile == 1:
        return stack([none, [first[0], zero], [zero, second[0]], none])
    return stack([none, none, [keep_low(first[1]), zero], [keep_high(second[1]), second[0]]])


def gather_heads(outs, g_t):
    main = jnp.concatenate([outs[0][:32, :128], outs[1][:32, :128], outs[1][32:, 128:], outs[2][32:, 128:]], axis=0)
    tail = jnp.concatenate([keep_low(outs[0][:32, 128:]), keep_high(outs[0][32:, 128:]),
                            keep_low(outs[2][:32, :128]), keep_high(outs[2][32:, :128])], axis=0)
    return (jnp.concatenate([main, tail], axis=1) * g_t).astype(BF16)


def merge_tail(res):
    return jnp.concatenate([res[:128], res[128:192] + res[192:]], axis=0)


def kernel(axis, group, z_ref, wp_s, wb_s, wo_s, wp_e, wb_e, wo_e, w1_ref, w2_ref, y_ref,
           wt_s, wt_e, row_bias, send_bias, got_bias, bias_t, normed_sc, q_sc, k_sc, v_sc, g_sc, gated_sc,
           send_h, got_h, send_d, got_d, flat,
           bias_send_sem, bias_recv_sem, h_send_sem, h_recv_sem, d_send_sem, d_recv_sem):
    rows, seq_len, channels = z_ref.shape
    pairs = rows // 2
    scale = 32 ** -0.5
    me = lax.axis_index(axis)
    peers = [lax.rem(me + step, group) for step in range(1, group)]

    barrier = pltpu.get_barrier_semaphore()
    for peer in peers:
        pl.semaphore_signal(barrier, inc=1, device_id={axis: peer}, device_id_type=MESH)

    for wp, wt in ((wp_s, wt_s), (wp_e, wt_e)):
        wt[0:channels] = wp[:, 0:channels].T
        wt[channels:2 * channels] = wp[:, 2 * channels:3 * channels].T
        wt[2 * channels:3 * channels] = wp[:, 3 * channels:].T

    def copy_bias(phase, peer):
        return pltpu.make_async_remote_copy(
            src_ref=send_bias.at[phase], dst_ref=got_bias.at[phase, me],
            send_sem=bias_send_sem.at[phase, peer], recv_sem=bias_recv_sem.at[phase, me],
            device_id={axis: peer}, device_id_type=MESH)

    def wait_bias(phase):
        for peer in peers:
            pltpu.make_async_copy(got_bias.at[phase, peer], got_bias.at[phase, peer], bias_recv_sem.at[phase, peer]).wait()

    def send_pair(send, got, send_sem, recv_sem, pair):
        for peer in peers:
            pltpu.make_async_remote_copy(
                src_ref=send.at[peer, pair], dst_ref=got.at[me, pair],
                send_sem=send_sem.at[peer], recv_sem=recv_sem.at[me],
                device_id={axis: peer}, device_id_type=MESH).start()

    def wait_all(got, recv_sem):
        for peer in peers:
            pltpu.make_async_copy(got.at[peer], got.at[peer], recv_sem.at[peer]).wait()

    def store_pair(send, got, pair, first, second):
        for dest in range(group):
            span = slice(rows * dest, rows * dest + rows)
            send[dest, pair] = jnp.concatenate([first[span], second[span]], axis=0).astype(BF16)
        got[me, pair] = send[me, pair]

    def publish_bias(phase):
        rounded = row_bias[...].astype(BF16)
        send_bias[phase] = rounded
        got_bias[phase, me] = rounded

    def project(slot, normed_dup, wt, wp):
        cols = dot(wt[...], normed_dup, 1, 1)
        keys = dot(normed_dup[:seq_len], wp[:, channels:2 * channels])
        return slot, cols, keys

    def stage(projected):
        slot, cols, keys = projected
        q_sc[slot] = cols[:channels].astype(BF16)
        v_sc[slot] = cols[channels:2 * channels, :seq_len].astype(BF16)
        g_sc[slot] = jax.nn.sigmoid(cols[2 * channels:])
        k_sc[slot] = keys.astype(BF16)

    class Attention:
        def __init__(self, slots):
            self.slots = slots
            self.score, self.prob, self.mixed, self.done = {}, {}, {}, {}

        def qk(self, unit):
            slot, tile = self.slots[unit // 3], unit % 3
            self.score[unit] = dot(k_sc[slot], score_block(q_sc[slot], tile))

        def soften(self, unit):
            tile = unit % 3
            scores = self.score.pop(unit) * scale + bias_t[:, 256 * tile:256 * tile + 256]
            top = jnp.max(scores, axis=0, keepdims=True)
            prob = jnp.exp(scores - top)
            self.prob[unit] = prob.astype(BF16), jnp.sum(prob, axis=0, keepdims=True)

        def mix(self, unit):
            slot, tile = self.slots[unit // 3], unit % 3
            prob, total = self.prob.pop(unit)
            self.mixed[unit] = dot(v_sc[slot, 32 * tile:32 * tile + 64], prob), total

        def norm(self, unit):
            mixed, total = self.mixed.pop(unit)
            self.done[unit] = mixed / total

        def gate(self, sub):
            outs = [self.done.pop(3 * sub + tile) for tile in range(3)]
            gated_sc[sub] = gather_heads(outs, g_sc[self.slots[sub]])

    def out_dot(sub, wo):
        return dot(gated_sc[sub].T, wo[...])

    batch = 4

    @pl.loop(0, rows // batch)
    def _(step):
        normed = [layer_norm(z_ref[step * batch + sub]) for sub in range(batch)]
        full = [dot(wb_s[...], duplicate_tail(val), 1, 1) for val in normed]
        for sub in range(batch):
            normed_sc[step * batch + sub] = normed[sub]
        for sub in range(batch):
            row_bias[pl.ds(step * batch + sub, 1), :] = bias_row(full[sub])

    publish_bias(0)
    pl.semaphore_wait(barrier, group - 1)
    for peer in peers:
        copy_bias(0, peer).start()

    @pl.loop(0, pairs)
    def _(step):
        made = [project(2 * step + sub, duplicate_tail(normed_sc[2 * step + sub]), wt_s, wp_s) for sub in range(2)]
        for val in made:
            stage(val)

    wait_bias(0)
    low = low_half((64, 128))
    by_query = jnp.concatenate([got_bias[0, src].astype(F32) for src in range(group)], axis=0)
    by_query = jnp.concatenate([by_query, by_query[128:]], axis=0)
    for first in (0, 1):
        base = 384 * first
        head_a = by_query[:, base:base + 128].T
        mixed = by_query[:, base + 128:base + 256].T
        head_b = by_query[:, base + 256:base + 384].T
        bias_t[0:128, base:base + 128] = head_a[:, :128]
        bias_t[128:192, base:base + 128] = mixed[:64, :128]
        low_a = low_half((128, 128))
        bias_t[0:128, base + 128:base + 256] = jnp.where(low_a, head_a[:, 128:], head_b[:, 128:])
        bias_t[128:192, base + 128:base + 256] = jnp.where(low, mixed[:64, 128:], mixed[64:, 128:])
        bias_t[0:128, base + 256:base + 384] = head_b[:, :128]
        bias_t[128:192, base + 256:base + 384] = mixed[64:, :128]

    def start_resid(pair, sub, res):
        row = 2 * pair + sub
        value = z_ref[row] + merge_tail(res)
        y_ref[row] = value
        return value, duplicate_tail(layer_norm(value.astype(BF16).astype(F32)))

    def start_tail(pair):
        res = [out_dot(sub, wo_s) for sub in range(2)]
        made = [start_resid(pair, sub, res[sub]) for sub in range(2)]
        full = [dot(wb_e[...], made[sub][1], 1, 1) for sub in range(2)]
        store_pair(send_h, got_h, pair, made[0][0], made[1][0])
        for sub in range(2):
            row_bias[pl.ds(2 * pair + sub, 1), :] = bias_row(full[sub])

    @pl.loop(0, pairs)
    def _(pair):
        @pl.when(pair > 1)
        def _():
            send_pair(send_h, got_h, h_send_sem, h_recv_sem, pair - 2)

        last = jnp.maximum(pair - 1, 0)
        att = Attention([2 * pair, 2 * pair + 1])
        att.qk(0)
        res = [out_dot(sub, wo_s) for sub in range(2)]
        att.qk(1)
        att.soften(0)
        att.mix(0)
        att.qk(2)
        made = [start_resid(last, 0, res[0])]
        att.soften(1)
        att.norm(0)
        att.mix(1)
        att.qk(3)
        made.append(start_resid(last, 1, res[1]))
        full = [dot(wb_e[...], made[0][1], 1, 1)]
        att.soften(2)
        att.norm(1)
        att.mix(2)
        att.qk(4)
        full.append(dot(wb_e[...], made[1][1], 1, 1))
        store_pair(send_h, got_h, last, made[0][0], made[1][0])
        att.soften(3)
        att.norm(2)
        att.mix(3)
        att.gate(0)
        att.qk(5)
        row_bias[pl.ds(2 * last, 1), :] = bias_row(full[0])
        att.soften(4)
        att.norm(3)
        att.mix(4)
        att.soften(5)
        att.norm(4)
        att.mix(5)
        row_bias[pl.ds(2 * last + 1, 1), :] = bias_row(full[1])
        att.norm(5)
        att.gate(1)

    send_pair(send_h, got_h, h_send_sem, h_recv_sem, pairs - 2)
    start_tail(pairs - 1)
    publish_bias(1)
    send_pair(send_h, got_h, h_send_sem, h_recv_sem, pairs - 1)
    for peer in peers:
        copy_bias(1, peer).start()

    wait_all(got_h, h_recv_sem)

    def spread(got):
        @pl.loop(0, group)
        def _(src):
            @pl.loop(0, pairs)
            def _(pair):
                start = pl.multiple_of((src * pairs + pair) * 2 * rows, 2 * rows)
                flat[pl.ds(start, 2 * rows), :] = got[src, pair].astype(F32)

    spread(got_h)

    def column(col):
        return flat[pl.ds(col, seq_len, stride=rows), :]

    for sub in range(2):
        stage(project(sub, duplicate_tail(layer_norm(column(sub))), wt_e, wp_e))

    wait_bias(1)
    for src in range(group):
        bias_t[rows * src:rows * src + rows] = got_bias[1, src].astype(F32)

    def end_mid(pair, sub, res):
        upd = merge_tail(res)
        return upd, layer_norm(column(2 * pair + sub) + upd)

    def widen(mid):
        return jnp.maximum(dot(mid[1], w1_ref[...]), 0.0).astype(BF16)

    def end_tail(pair):
        res = [out_dot(sub, wo_e) for sub in range(2)]
        mids = [end_mid(pair, sub, res[sub]) for sub in range(2)]
        hidden = [widen(mid) for mid in mids]
        delta = [mids[sub][0] + dot(hidden[sub], w2_ref[...]) for sub in range(2)]
        store_pair(send_d, got_d, pair, delta[0], delta[1])

    @pl.loop(0, pairs)
    def _(pair):
        @pl.when(pair > 1)
        def _():
            send_pair(send_d, got_d, d_send_sem, d_recv_sem, pair - 2)

        last = jnp.maximum(pair - 1, 0)
        ahead = jnp.minimum(pair + 1, pairs - 1)
        here = 2 * lax.rem(pair, 2)
        there = 2 - here
        att = Attention([here, here + 1])
        att.qk(0)
        res = [out_dot(sub, wo_e) for sub in range(2)]
        att.qk(1)
        normed = [duplicate_tail(layer_norm(column(2 * ahead + sub))) for sub in range(2)]
        att.soften(0)
        att.mix(0)
        made = project(there, normed[0], wt_e, wp_e)
        att.qk(2)
        mids = [end_mid(last, 0, res[0])]
        att.soften(1)
        att.norm(0)
        att.mix(1)
        stage(made)
        att.qk(3)
        mids.append(end_mid(last, 1, res[1]))
        hidden = [widen(mids[0])]
        att.soften(2)
        att.norm(1)
        att.mix(2)
        hidden.append(widen(mids[1]))
        att.qk(4)
        delta = [mids[0][0] + dot(hidden[0], w2_ref[...])]
        att.soften(3)
        att.norm(2)
        att.gate(0)
        att.mix(3)
        delta.append(mids[1][0] + dot(hidden[1], w2_ref[...]))
        att.qk(5)
        made = project(there + 1, normed[1], wt_e, wp_e)
        att.soften(4)
        att.norm(3)
        att.mix(4)
        stage(made)
        store_pair(send_d, got_d, last, delta[0], delta[1])
        att.soften(5)
        att.norm(4)
        att.mix(5)
        att.norm(5)
        att.gate(1)

    send_pair(send_d, got_d, d_send_sem, d_recv_sem, pairs - 2)
    end_tail(pairs - 1)
    send_pair(send_d, got_d, d_send_sem, d_recv_sem, pairs - 1)

    wait_all(got_d, d_recv_sem)
    spread(got_d)

    @pl.loop(0, rows)
    def _(row):
        y_ref[row] = y_ref[row] + column(row)

    for peer in peers:
        for phase in range(2):
            pltpu.make_async_copy(send_bias.at[phase], send_bias.at[phase], bias_send_sem.at[phase, peer]).wait()
        pltpu.make_async_copy(send_h.at[peer], send_h.at[peer], h_send_sem.at[peer]).wait()
        pltpu.make_async_copy(send_d.at[peer], send_d.at[peer], d_send_sem.at[peer]).wait()


def solution(mesh):
    row_spec = P(('dp', 'sp'), None, None)
    group = mesh.shape['sp']

    def local_fn(pair_loc, w_qkvg_s, w_bias_s, w_out_s, w_qkvg_e, w_bias_e, w_out_e, w_one, w_two):
        rows, seq_len, channels = pair_loc.shape
        heads = w_bias_s.shape[0]
        pairs = rows // 2
        vmem = pl.BlockSpec(memory_space=pltpu.VMEM)
        wide = heads * seq_len
        exchange = pltpu.VMEM((group, pairs, 2 * rows, channels), BF16)
        return pl.pallas_call(
            functools.partial(kernel, 'sp', group),
            out_shape=jax.ShapeDtypeStruct(pair_loc.shape, F32),
            in_specs=[vmem] * 9,
            out_specs=vmem,
            scratch_shapes=[
                pltpu.VMEM((3 * channels, channels), BF16),
                pltpu.VMEM((3 * channels, channels), BF16),
                pltpu.VMEM((rows, wide), F32),
                pltpu.VMEM((2, rows, wide), BF16),
                pltpu.VMEM((2, group, rows, wide), BF16),
                pltpu.VMEM((seq_len, wide), F32),
                pltpu.VMEM((rows, seq_len, channels), BF16),
                pltpu.VMEM((rows, channels, 256), BF16),
                pltpu.VMEM((rows, seq_len, channels), BF16),
                pltpu.VMEM((rows, channels, seq_len), BF16),
                pltpu.VMEM((rows, channels, 256), F32),
                pltpu.VMEM((2, channels, 256), BF16),
                exchange, exchange, exchange, exchange,
                pltpu.VMEM((rows * seq_len, channels), F32),
                pltpu.SemaphoreType.DMA((2, group)),
                pltpu.SemaphoreType.DMA((2, group)),
                pltpu.SemaphoreType.DMA((group,)),
                pltpu.SemaphoreType.DMA((group,)),
                pltpu.SemaphoreType.DMA((group,)),
                pltpu.SemaphoreType.DMA((group,)),
            ],
            compiler_params=pltpu.CompilerParams(collective_id=0, has_side_effects=True, vmem_limit_bytes=60 * 1024 * 1024),
        )(pair_loc, w_qkvg_s, w_bias_s, w_out_s, w_qkvg_e, w_bias_e, w_out_e, w_one, w_two)

    return jax.shard_map(local_fn, mesh=mesh, in_specs=(row_spec, P(), P(), P(), P(), P(), P(), P(), P()), out_specs=row_spec, check_vma=False)
```

time: 110 us -> 59.6 us (0.54)
  Pallas kernels: 106 us -> 55.9 us
    pallas_call x1, Pallas kernels: 106 us -> 55.9 us  [local_fn(): pl.pallas_call(functools.partial(kernel, 'sp', group), out_shape=jax.Shap...]
where the time goes in v2:
time: 59.6 us; the launch traced here: 59.2 us
  Pallas kernels  55.9 us (94%)
  local copies, waits for them, and re-layouts  3.3 us (6%)
    pallas_call x1, Pallas kernels, local_fn(): pl.pallas_call(functools.partial(kernel, 'sp', group), out_shape=jax.Shap...  55.9 us
    unnamed x1, local copies, waits for them, and re-layouts  3.3 us

profile of v2, /device:TPU:112, one launch (start us, length us, event | category | flops | bytes accessed | tf_op | source)
XLA Modules:
  0.0 59.2 jit_solution(1123204556902763209)
XLA Ops:
  0.0 55.9 %shard_map.91 = f32[24,192,128]{2,1,0:T(8,128)} custom-call(f32[24,192,128]{2,1,0:T(8,128)} %z_ref.1, bf16[128,512]{1,0:T(8,128)(2,1)} %wp_s.1, bf16[4,128]{1,0:T(4,128)(2,1)} %wb_s.1, bf16[128,128]{1,0:T(8,128)(2,1)} %wo_s.1, bf16[128,512]{1,0:T(8,128)(2,1)} %wp_e.1, bf16[4,128]{1,0:T(4,128)(2,1)} %wb_e.1, bf16[128,128]{1,0:T(8,128)(2,1)} %wo_e.1, ...), custom_call_target="tpu_custom_call" | custom-call | tf_op jit(solution)/shard_map/pallas_call | solution.py:396
  55.9 3.3 %copy.11 = f32[24,192,128]{2,1,0:T(8,128)} copy(f32[24,192,128]{2,1,0:T(8,128)} %shard_map.91) | data formatting | bytes 4718592

commit v3 on v2

--- a/solution.py
+++ b/solution.py
@@ -79,12 +79,17 @@
     return jnp.concatenate([res[:128], res[128:192] + res[192:]], axis=0)
 
 
-def kernel(axis, group, z_ref, wp_s, wb_s, wo_s, wp_e, wb_e, wo_e, w1_ref, w2_ref, y_ref,
+def kernel(axis, group, early, z_hbm, wp_s_hbm, wb_s_hbm, wo_s_hbm, wp_e_hbm, wb_e_hbm, wo_e_hbm, w1_hbm, w2_hbm, y_ref,
+           z_ref, wp_s, wb_s, wo_s, wp_e, wb_e, wo_e, w1_ref, w2_ref,
            wt_s, wt_e, row_bias, send_bias, got_bias, bias_t, normed_sc, q_sc, k_sc, v_sc, g_sc, gated_sc,
-           send_h, got_h, send_d, got_d, flat,
-           bias_send_sem, bias_recv_sem, h_send_sem, h_recv_sem, d_send_sem, d_recv_sem):
-    rows, seq_len, channels = z_ref.shape
+           send_first, got_first, send_rest, got_rest, send_d, got_d, flat,
+           z_sem, w_sem, bias_send_sem, bias_recv_sem, first_send_sem, first_recv_sem, rest_send_sem, rest_recv_sem,
+           d_send_sem, d_recv_sem):
+    rows, seq_len, channels = z_hbm.shape
     pairs = rows // 2
+    chunk = 8
+    chunks = rows // chunk
+    late = 2 * pairs // 3
     scale = 32 ** -0.5
     me = lax.axis_index(axis)
     peers = [lax.rem(me + step, group) for step in range(1, group)]
@@ -93,42 +98,66 @@
     for peer in peers:
         pl.semaphore_signal(barrier, inc=1, device_id={axis: peer}, device_id_type=MESH)
 
-    for wp, wt in ((wp_s, wt_s), (wp_e, wt_e)):
-        wt[0:channels] = wp[:, 0:channels].T
-        wt[channels:2 * channels] = wp[:, 2 * channels:3 * channels].T
-        wt[2 * channels:3 * channels] = wp[:, 3 * channels:].T
-
-    def copy_bias(phase, peer):
+    def load_z(idx):
+        span = pl.ds(idx * chunk, chunk)
+        return pltpu.make_async_copy(z_hbm.at[span], z_ref.at[span], z_sem.at[idx])
+
+    loads = [pltpu.make_async_copy(src, dst, w_sem.at[idx]) for idx, (src, dst) in enumerate(
+        ((wb_s_hbm, wb_s), (wp_s_hbm, wp_s), (wp_e_hbm, wp_e), (wo_s_hbm, wo_s), (wb_e_hbm, wb_e),
+         (wo_e_hbm, wo_e), (w1_hbm, w1_ref), (w2_hbm, w2_ref)))]
+    load_z(0).start()
+    loads[0].start()
+    loads[1].start()
+    for idx in range(1, chunks):
+        load_z(idx).start()
+    for load in loads[2:]:
+        load.start()
+
+    def copy_bias(phase, part, peer):
         return pltpu.make_async_remote_copy(
-            src_ref=send_bias.at[phase], dst_ref=got_bias.at[phase, me],
+            src_ref=send_bias.at[phase, part], dst_ref=got_bias.at[phase, me, part],
             send_sem=bias_send_sem.at[phase, peer], recv_sem=bias_recv_sem.at[phase, me],
             device_id={axis: peer}, device_id_type=MESH)
+
+    def send_bias_part(phase, part):
+        for peer in peers:
+            copy_bias(phase, part, peer).start()
+
+    def publish_bias(phase, part):
+        rounded = row_bias[chunk * part:chunk * part + chunk].astype(BF16)
+        send_bias[phase, part] = rounded
+        got_bias[phase, me, part] = rounded
 
     def wait_bias(phase):
         for peer in peers:
             pltpu.make_async_copy(got_bias.at[phase, peer], got_bias.at[phase, peer], bias_recv_sem.at[phase, peer]).wait()
 
-    def send_pair(send, got, send_sem, recv_sem, pair):
+    def send_blocks(send, got, send_sem, recv_sem, start, count):
+        span = pl.ds(start, count)
         for peer in peers:
             pltpu.make_async_remote_copy(
-                src_ref=send.at[peer, pair], dst_ref=got.at[me, pair],
+                src_ref=send.at[peer, span], dst_ref=got.at[me, span],
                 send_sem=send_sem.at[peer], recv_sem=recv_sem.at[me],
                 device_id={axis: peer}, device_id_type=MESH).start()
+
+    def send_early(start, count):
+        send_blocks(send_first, got_first, first_send_sem, first_recv_sem, start, count)
+
+    def send_later(start, count):
+        send_blocks(send_rest, got_rest, rest_send_sem, rest_recv_sem, start, count)
+
+    def send_delta(pair):
+        send_blocks(send_d, got_d, d_send_sem, d_recv_sem.at[pair // late], pair, 1)
 
     def wait_all(got, recv_sem):
         for peer in peers:
             pltpu.make_async_copy(got.at[peer], got.at[peer], recv_sem.at[peer]).wait()
 
-    def store_pair(send, got, pair, first, second):
+    def store_block(send, got, pair, first, second, low, high):
         for dest in range(group):
-            span = slice(rows * dest, rows * dest + rows)
+            span = slice(rows * dest + low, rows * dest + high)
             send[dest, pair] = jnp.concatenate([first[span], second[span]], axis=0).astype(BF16)
         got[me, pair] = send[me, pair]
-
-    def publish_bias(phase):
-        rounded = row_bias[...].astype(BF16)
-        send_bias[phase] = rounded
-        got_bias[phase, me] = rounded
 
     def project(slot, normed_dup, wt, wp):
         cols = dot(wt[...], normed_dup, 1, 1)
@@ -142,6 +171,11 @@
         g_sc[slot] = jax.nn.sigmoid(cols[2 * channels:])
         k_sc[slot] = keys.astype(BF16)
 
+    def transpose_weights(wp, wt):
+        wt[0:channels] = wp[:, 0:channels].T
+        wt[channels:2 * channels] = wp[:, 2 * channels:3 * channels].T
+        wt[2 * channels:3 * channels] = wp[:, 3 * channels:].T
+
     class Attention:
         def __init__(self, slots):
             self.slots = slots
@@ -175,20 +209,34 @@
         return dot(gated_sc[sub].T, wo[...])
 
     batch = 4
-
-    @pl.loop(0, rows // batch)
-    def _(step):
-        normed = [layer_norm(z_ref[step * batch + sub]) for sub in range(batch)]
-        full = [dot(wb_s[...], duplicate_tail(val), 1, 1) for val in normed]
-        for sub in range(batch):
-            normed_sc[step * batch + sub] = normed[sub]
-        for sub in range(batch):
-            row_bias[pl.ds(step * batch + sub, 1), :] = bias_row(full[sub])
-
-    publish_bias(0)
-    pl.semaphore_wait(barrier, group - 1)
-    for peer in peers:
-        copy_bias(0, peer).start()
+    loads[0].wait()
+    for part in range(chunks):
+        load_z(part).wait()
+
+        @pl.loop(0, chunk // batch)
+        def _(step):
+            base = chunk * part + step * batch
+            normed = [layer_norm(z_ref[base + sub]) for sub in range(batch)]
+            full = [dot(wb_s[...], duplicate_tail(val), 1, 1) for val in normed]
+            for sub in range(batch):
+                normed_sc[base + sub] = normed[sub]
+            for sub in range(batch):
+                row_bias[pl.ds(base + sub, 1), :] = bias_row(full[sub])
+
+        publish_bias(0, part)
+        if part == 0:
+            loads[1].wait()
+            transpose_weights(wp_s, wt_s)
+            pl.semaphore_wait(barrier, group - 1)
+        if part == 1:
+            loads[2].wait()
+            transpose_weights(wp_e, wt_e)
+        if part == 2:
+            stage(project(0, duplicate_tail(normed_sc[0]), wt_s, wp_s))
+        send_bias_part(0, part)
+
+    for load in loads[3:]:
+        load.wait()
 
     @pl.loop(0, pairs)
     def _(step):
@@ -196,9 +244,12 @@
         for val in made:
             stage(val)
 
+    def bias_of(phase, src):
+        return jnp.concatenate([got_bias[phase, src, part].astype(F32) for part in range(chunks)], axis=0)
+
     wait_bias(0)
     low = low_half((64, 128))
-    by_query = jnp.concatenate([got_bias[0, src].astype(F32) for src in range(group)], axis=0)
+    by_query = jnp.concatenate([bias_of(0, src) for src in range(group)], axis=0)
     by_query = jnp.concatenate([by_query, by_query[128:]], axis=0)
     for first in (0, 1):
         base = 384 * first
@@ -219,19 +270,36 @@
         y_ref[row] = value
         return value, duplicate_tail(layer_norm(value.astype(BF16).astype(F32)))
 
+    def store_h(pair, first, second):
+        store_block(send_first, got_first, pair, first, second, 0, early)
+        store_block(send_rest, got_rest, pair, first, second, early, rows)
+
     def start_tail(pair):
         res = [out_dot(sub, wo_s) for sub in range(2)]
         made = [start_resid(pair, sub, res[sub]) for sub in range(2)]
         full = [dot(wb_e[...], made[sub][1], 1, 1) for sub in range(2)]
-        store_pair(send_h, got_h, pair, made[0][0], made[1][0])
+        store_h(pair, made[0][0], made[1][0])
         for sub in range(2):
             row_bias[pl.ds(2 * pair + sub, 1), :] = bias_row(full[sub])
 
     @pl.loop(0, pairs)
     def _(pair):
-        @pl.when(pair > 1)
+        @pl.when(jnp.logical_and(pair > 2, lax.rem(pair, 2) == 1))
         def _():
-            send_pair(send_h, got_h, h_send_sem, h_recv_sem, pair - 2)
+            send_early(pair - 3, 2)
+
+        @pl.when(jnp.logical_and(pair > 4, lax.rem(pair, 2) == 1))
+        def _():
+            send_later(pair - 5, 2)
+
+        for part in range(chunks - 1):
+            @pl.when(pair == (part + 1) * (chunk // 2) + 1)
+            def _():
+                publish_bias(1, part)
+
+            @pl.when(pair == (part + 1) * (chunk // 2) + 2)
+            def _():
+                send_bias_part(1, part)
 
         last = jnp.maximum(pair - 1, 0)
         att = Attention([2 * pair, 2 * pair + 1])
@@ -253,7 +321,7 @@
         att.mix(2)
         att.qk(4)
         full.append(dot(wb_e[...], made[1][1], 1, 1))
-        store_pair(send_h, got_h, last, made[0][0], made[1][0])
+        store_h(last, made[0][0], made[1][0])
         att.soften(3)
         att.norm(2)
         att.mix(3)
@@ -270,34 +338,36 @@
         att.norm(5)
         att.gate(1)
 
-    send_pair(send_h, got_h, h_send_sem, h_recv_sem, pairs - 2)
     start_tail(pairs - 1)
-    publish_bias(1)
-    send_pair(send_h, got_h, h_send_sem, h_recv_sem, pairs - 1)
-    for peer in peers:
-        copy_bias(1, peer).start()
-
-    wait_all(got_h, h_recv_sem)
-
-    def spread(got):
+    publish_bias(1, chunks - 1)
+    send_early(pairs - 2, 2)
+    send_bias_part(1, chunks - 1)
+    send_later(pairs - 4, 4)
+
+    def spread(got, low, high):
+        width = high - low
+
         @pl.loop(0, group)
         def _(src):
             @pl.loop(0, pairs)
             def _(pair):
-                start = pl.multiple_of((src * pairs + pair) * 2 * rows, 2 * rows)
-                flat[pl.ds(start, 2 * rows), :] = got[src, pair].astype(F32)
-
-    spread(got_h)
+                block = got[src, pair].astype(F32)
+                for sub in range(2):
+                    start = pl.multiple_of(((src * pairs + pair) * 2 + sub) * rows + low, 8)
+                    flat[pl.ds(start, width), :] = block[width * sub:width * sub + width]
 
     def column(col):
         return flat[pl.ds(col, seq_len, stride=rows), :]
 
+    wait_all(got_first, first_recv_sem)
+    spread(got_first, 0, early)
+
     for sub in range(2):
         stage(project(sub, duplicate_tail(layer_norm(column(sub))), wt_e, wp_e))
 
     wait_bias(1)
     for src in range(group):
-        bias_t[rows * src:rows * src + rows] = got_bias[1, src].astype(F32)
+        bias_t[rows * src:rows * src + rows] = bias_of(1, src)
 
     def end_mid(pair, sub, res):
         upd = merge_tail(res)
@@ -311,13 +381,18 @@
         mids = [end_mid(pair, sub, res[sub]) for sub in range(2)]
         hidden = [widen(mid) for mid in mids]
         delta = [mids[sub][0] + dot(hidden[sub], w2_ref[...]) for sub in range(2)]
-        store_pair(send_d, got_d, pair, delta[0], delta[1])
+        store_block(send_d, got_d, pair, delta[0], delta[1], 0, rows)
 
     @pl.loop(0, pairs)
     def _(pair):
+        @pl.when(pair == early // 2 - 1)
+        def _():
+            wait_all(got_rest, rest_recv_sem)
+            spread(got_rest, early, rows)
+
         @pl.when(pair > 1)
         def _():
-            send_pair(send_d, got_d, d_send_sem, d_recv_sem, pair - 2)
+            send_delta(pair - 2)
 
         last = jnp.maximum(pair - 1, 0)
         ahead = jnp.minimum(pair + 1, pairs - 1)
@@ -357,53 +432,76 @@
         att.norm(3)
         att.mix(4)
         stage(made)
-        store_pair(send_d, got_d, last, delta[0], delta[1])
+        store_block(send_d, got_d, last, delta[0], delta[1], 0, rows)
         att.soften(5)
         att.norm(4)
         att.mix(5)
         att.norm(5)
         att.gate(1)
 
-    send_pair(send_d, got_d, d_send_sem, d_recv_sem, pairs - 2)
+    send_delta(pairs - 2)
     end_tail(pairs - 1)
-    send_pair(send_d, got_d, d_send_sem, d_recv_sem, pairs - 1)
-
-    wait_all(got_d, d_recv_sem)
-    spread(got_d)
-
-    @pl.loop(0, rows)
-    def _(row):
-        y_ref[row] = y_ref[row] + column(row)
+    send_delta(pairs - 1)
+
+    def finish(part, first, count):
+        span = pl.ds(first, count)
+        for peer in peers:
+            pltpu.make_async_copy(got_d.at[peer, span], got_d.at[peer, span], d_recv_sem.at[part, peer]).wait()
+
+        @pl.loop(0, group)
+        def _(src):
+            @pl.loop(first, first + count)
+            def _(pair):
+                start = pl.multiple_of((src * pairs + pair) * 2 * rows, 2 * rows)
+                flat[pl.ds(start, 2 * rows), :] = got_d[src, pair].astype(F32)
+
+        @pl.loop(0, rows)
+        def _(row):
+            for src in range(group):
+                low_col = rows * src + 2 * first
+                y_ref[row, low_col:low_col + 2 * count] += flat[pl.ds(low_col * rows + row, 2 * count, stride=rows), :]
+
+    finish(0, 0, late)
+    finish(1, late, pairs - late)
+
+    def drain(ref, sem):
+        pltpu.make_async_copy(ref, ref, sem).wait()
 
     for peer in peers:
         for phase in range(2):
-            pltpu.make_async_copy(send_bias.at[phase], send_bias.at[phase], bias_send_sem.at[phase, peer]).wait()
-        pltpu.make_async_copy(send_h.at[peer], send_h.at[peer], h_send_sem.at[peer]).wait()
-        pltpu.make_async_copy(send_d.at[peer], send_d.at[peer], d_send_sem.at[peer]).wait()
+            drain(send_bias.at[phase], bias_send_sem.at[phase, peer])
+        drain(send_first.at[peer], first_send_sem.at[peer])
+        drain(send_rest.at[peer], rest_send_sem.at[peer])
+        drain(send_d.at[peer], d_send_sem.at[peer])
 
 
 def solution(mesh):
     row_spec = P(('dp', 'sp'), None, None)
     group = mesh.shape['sp']
 
-    def local_fn(pair_loc, w_qkvg_s, w_bias_s, w_out_s, w_qkvg_e, w_bias_e, w_out_e, w_one, w_two):
+    def local_fn(pair_loc, *weights):
         rows, seq_len, channels = pair_loc.shape
-        heads = w_bias_s.shape[0]
+        heads = weights[1].shape[0]
         pairs = rows // 2
-        vmem = pl.BlockSpec(memory_space=pltpu.VMEM)
         wide = heads * seq_len
-        exchange = pltpu.VMEM((group, pairs, 2 * rows, channels), BF16)
+        early = 8
+        chunk = 8
+        hbm = pl.BlockSpec(memory_space=pltpu.HBM)
+
+        def exchange(width):
+            return pltpu.VMEM((group, pairs, 2 * width, channels), BF16)
+
         return pl.pallas_call(
-            functools.partial(kernel, 'sp', group),
+            functools.partial(kernel, 'sp', group, early),
             out_shape=jax.ShapeDtypeStruct(pair_loc.shape, F32),
-            in_specs=[vmem] * 9,
-            out_specs=vmem,
-            scratch_shapes=[
+            in_specs=[hbm] * 9,
+            out_specs=pl.BlockSpec(memory_space=pltpu.VMEM),
+            scratch_shapes=[pltpu.VMEM(pair_loc.shape, F32)] + [pltpu.VMEM(val.shape, BF16) for val in weights] + [
                 pltpu.VMEM((3 * channels, channels), BF16),
                 pltpu.VMEM((3 * channels, channels), BF16),
                 pltpu.VMEM((rows, wide), F32),
-                pltpu.VMEM((2, rows, wide), BF16),
-                pltpu.VMEM((2, group, rows, wide), BF16),
+                pltpu.VMEM((2, rows // chunk, chunk, wide), BF16),
+                pltpu.VMEM((2, group, rows // chunk, chunk, wide), BF16),
                 pltpu.VMEM((seq_len, wide), F32),
                 pltpu.VMEM((rows, seq_len, channels), BF16),
                 pltpu.VMEM((rows, channels, 256), BF16),
@@ -411,16 +509,20 @@
                 pltpu.VMEM((rows, channels, seq_len), BF16),
                 pltpu.VMEM((rows, channels, 256), F32),
                 pltpu.VMEM((2, channels, 256), BF16),
-                exchange, exchange, exchange, exchange,
+                exchange(early), exchange(early), exchange(rows - early), exchange(rows - early), exchange(rows), exchange(rows),
                 pltpu.VMEM((rows * seq_len, channels), F32),
+                pltpu.SemaphoreType.DMA((rows // chunk,)),
+                pltpu.SemaphoreType.DMA((8,)),
                 pltpu.SemaphoreType.DMA((2, group)),
                 pltpu.SemaphoreType.DMA((2, group)),
                 pltpu.SemaphoreType.DMA((group,)),
                 pltpu.SemaphoreType.DMA((group,)),
                 pltpu.SemaphoreType.DMA((group,)),
                 pltpu.SemaphoreType.DMA((group,)),
+                pltpu.SemaphoreType.DMA((group,)),
+                pltpu.SemaphoreType.DMA((2, group)),
             ],
-            compiler_params=pltpu.CompilerParams(collective_id=0, has_side_effects=True, vmem_limit_bytes=60 * 1024 * 1024),
-        )(pair_loc, w_qkvg_s, w_bias_s, w_out_s, w_qkvg_e, w_bias_e, w_out_e, w_one, w_two)
+            compiler_params=pltpu.CompilerParams(collective_id=0, has_side_effects=True, vmem_limit_bytes=34 * 1024 * 1024),
+        )(*[pltpu.with_memory_space_constraint(val, pltpu.HBM) for val in (pair_loc, *weights)])
 
     return jax.shard_map(local_fn, mesh=mesh, in_specs=(row_spec, P(), P(), P(), P(), P(), P(), P(), P()), out_specs=row_spec, check_vma=False)

time: 59.6 us -> 55.4 us (0.930)
  Pallas kernels: 55.9 us -> 53.6 us
  local copies, waits for them, and re-layouts: 3.3 us -> 1.41 us
    pallas_call x1, Pallas kernels: 55.9 us -> 53.6 us  [local_fn(): pl.pallas_call(functools.partial(kernel, 'sp', group, early), out_shape=j...]
    unnamed x1, local copies, waits for them, and re-layouts: 3.3 us -> 1.41 us
where the time goes in v3:
time: 55.4 us; the launch traced here: 55 us
  Pallas kernels  53.6 us (97%)
  local copies, waits for them, and re-layouts  1.41 us (3%)
    pallas_call x1, Pallas kernels, local_fn(): pl.pallas_call(functools.partial(kernel, 'sp', group, early), out_shape=j...  53.6 us
    unnamed x1, local copies, waits for them, and re-layouts  1.41 us

profile of v3, /device:TPU:112, one launch (start us, length us, event | category | flops | bytes accessed | tf_op | source)
XLA Modules:
  0.0 55.0 jit_solution(15014109683432717731)
XLA Ops:
  0.0 53.6 %shard_map.91 = f32[24,192,128]{2,1,0:T(8,128)S(1)} custom-call(f32[24,192,128]{2,1,0:T(8,128)} %z_hbm.1, bf16[128,512]{1,0:T(8,128)(2,1)} %wp_s_hbm.1, bf16[4,128]{1,0:T(4,128)(2,1)} %wb_s_hbm.1, bf16[128,128]{1,0:T(8,128)(2,1)} %wo_s_hbm.1, bf16[128,512]{1,0:T(8,128)(2,1)} %wp_e_hbm.1, bf16[4,128]{1,0:T(4,128)(2,1)} %wb_e_hbm.1, ...), custom_call_target="tpu_custom_call" | custom-call | tf_op jit(solution)/shard_map/pallas_call | solution.py:494
  53.6 1.4 %copy.11 = f32[24,192,128]{2,1,0:T(8,128)} copy(f32[24,192,128]{2,1,0:T(8,128)S(1)} %shard_map.91) | data formatting | bytes 4718592

commit v4 on v3

--- a/solution.py
+++ b/solution.py
@@ -8,6 +8,9 @@
 from jax.sharding import PartitionSpec as P
 
 LN_EPS = 1e-5
+Q_SHRINK = 0.125
+SHRINK = 32 ** -0.5 / Q_SHRINK
+LOG2_E = 1.4426950408889634
 MESH = pl.DeviceIdType.MESH
 F32 = jnp.float32
 BF16 = jnp.bfloat16
@@ -81,18 +84,24 @@
 
 def kernel(axis, group, early, z_hbm, wp_s_hbm, wb_s_hbm, wo_s_hbm, wp_e_hbm, wb_e_hbm, wo_e_hbm, w1_hbm, w2_hbm, y_ref,
            z_ref, wp_s, wb_s, wo_s, wp_e, wb_e, wo_e, w1_ref, w2_ref,
-           wt_s, wt_e, row_bias, send_bias, got_bias, bias_t, normed_sc, q_sc, k_sc, v_sc, g_sc, gated_sc,
+           wt_s, wt_e, row_bias, send_bias, got_bias, bias_t, normed_sc, q_sc, k_sc, v_sc, g_sc, gated_sc, part_sc, top_sc,
            send_first, got_first, send_rest, got_rest, send_d, got_d, flat,
-           z_sem, w_sem, bias_send_sem, bias_recv_sem, first_send_sem, first_recv_sem, rest_send_sem, rest_recv_sem,
+           z_sem, w_sem, bias_send_sem, bias_recv_sem, pass_send_sem, first_send_sem, first_recv_sem, rest_send_sem, rest_recv_sem,
            d_send_sem, d_recv_sem):
     rows, seq_len, channels = z_hbm.shape
     pairs = rows // 2
     chunk = 8
     chunks = rows // chunk
-    late = 2 * pairs // 3
-    scale = 32 ** -0.5
+    late = pairs - 3
+    later = rows // early - 1
+    held = pairs - 7
     me = lax.axis_index(axis)
-    peers = [lax.rem(me + step, group) for step in range(1, group)]
+    half = group // 2
+    order = sorted(range(1, group), key=lambda step: abs(step - half))
+    peers = [lax.rem(me + step, group) for step in order]
+    partner = me + 1 - 2 * lax.rem(me, 2)
+    alike = [lax.rem(me + step, group) for step in order if step % 2 == 0]
+    others = [lax.rem(partner + step, group) for step in order if step % 2 == 0]
 
     barrier = pltpu.get_barrier_semaphore()
     for peer in peers:
@@ -113,15 +122,24 @@
     for load in loads[2:]:
         load.start()
 
-    def copy_bias(phase, part, peer):
-        return pltpu.make_async_remote_copy(
-            src_ref=send_bias.at[phase, part], dst_ref=got_bias.at[phase, me, part],
-            send_sem=bias_send_sem.at[phase, peer], recv_sem=bias_recv_sem.at[phase, me],
-            device_id={axis: peer}, device_id_type=MESH)
-
-    def send_bias_part(phase, part):
-        for peer in peers:
-            copy_bias(phase, part, peer).start()
+    def send_bias_part(phase, part, count=1):
+        span = pl.ds(part, count)
+        for peer in peers if phase == 0 else alike + [partner]:
+            pltpu.make_async_remote_copy(
+                src_ref=send_bias.at[phase, span], dst_ref=got_bias.at[phase, me, span],
+                send_sem=bias_send_sem.at[phase, peer], recv_sem=bias_recv_sem.at[phase, me],
+                device_id={axis: peer}, device_id_type=MESH).start()
+
+    def wait_for_bias(phase, src):
+        pltpu.make_async_copy(got_bias.at[phase, src], got_bias.at[phase, src], bias_recv_sem.at[phase, src]).wait()
+
+    def forward_bias(phase):
+        for src in alike:
+            wait_for_bias(phase, src)
+            pltpu.make_async_remote_copy(
+                src_ref=got_bias.at[phase, src], dst_ref=got_bias.at[phase, src],
+                send_sem=pass_send_sem.at[src], recv_sem=bias_recv_sem.at[phase, src],
+                device_id={axis: partner}, device_id_type=MESH).start()
 
     def publish_bias(phase, part):
         rounded = row_bias[chunk * part:chunk * part + chunk].astype(BF16)
@@ -129,8 +147,8 @@
         got_bias[phase, me, part] = rounded
 
     def wait_bias(phase):
-        for peer in peers:
-            pltpu.make_async_copy(got_bias.at[phase, peer], got_bias.at[phase, peer], bias_recv_sem.at[phase, peer]).wait()
+        for src in peers if phase == 0 else [partner] + others:
+            wait_for_bias(phase, src)
 
     def send_blocks(send, got, send_sem, recv_sem, start, count):
         span = pl.ds(start, count)
@@ -141,17 +159,26 @@
                 device_id={axis: peer}, device_id_type=MESH).start()
 
     def send_early(start, count):
-        send_blocks(send_first, got_first, first_send_sem, first_recv_sem, start, count)
+        send_blocks(send_first, got_first, first_send_sem, first_recv_sem.at[int(isinstance(start, int) and start == pairs - 1)], start, count)
 
     def send_later(start, count):
-        send_blocks(send_rest, got_rest, rest_send_sem, rest_recv_sem, start, count)
-
-    def send_delta(pair):
-        send_blocks(send_d, got_d, d_send_sem, d_recv_sem.at[pair // late], pair, 1)
-
-    def wait_all(got, recv_sem):
+        span = pl.ds(start, count)
         for peer in peers:
-            pltpu.make_async_copy(got.at[peer], got.at[peer], recv_sem.at[peer]).wait()
+            pltpu.make_async_remote_copy(
+                src_ref=send_rest.at[peer, :, span], dst_ref=got_rest.at[me, :, span],
+                send_sem=rest_send_sem.at[0, peer], recv_sem=rest_recv_sem.at[0, me],
+                device_id={axis: peer}, device_id_type=MESH).start()
+
+    def send_last(idx, start, count):
+        span = pl.ds(start, count)
+        for peer in peers:
+            pltpu.make_async_remote_copy(
+                src_ref=send_rest.at[peer, idx, span], dst_ref=got_rest.at[me, idx, span],
+                send_sem=rest_send_sem.at[1 + idx, peer], recv_sem=rest_recv_sem.at[1 + idx, me],
+                device_id={axis: peer}, device_id_type=MESH).start()
+
+    def send_delta(start, count):
+        send_blocks(send_d, got_d, d_send_sem, d_recv_sem.at[start // late], start, count)
 
     def store_block(send, got, pair, first, second, low, high):
         for dest in range(group):
@@ -172,7 +199,7 @@
         k_sc[slot] = keys.astype(BF16)
 
     def transpose_weights(wp, wt):
-        wt[0:channels] = wp[:, 0:channels].T
+        wt[0:channels] = wp[:, 0:channels].T * jnp.asarray(Q_SHRINK, BF16)
         wt[channels:2 * channels] = wp[:, 2 * channels:3 * channels].T
         wt[2 * channels:3 * channels] = wp[:, 3 * channels:].T
 
@@ -185,12 +212,28 @@
             slot, tile = self.slots[unit // 3], unit % 3
             self.score[unit] = dot(k_sc[slot], score_block(q_sc[slot], tile))
 
+        def biased(self, unit, half):
+            at = 256 * (unit % 3) + 128 * half
+            return self.score[unit][:, 128 * half:128 * half + 128] + bias_t[:, at:at + 128]
+
+        def hand_on(self, unit):
+            for half in range(2):
+                part = self.biased(unit, half)
+                part_sc[unit % 3, half] = part
+                top_sc[unit % 3, half] = jnp.max(part, axis=0, keepdims=True)
+
         def soften(self, unit):
-            tile = unit % 3
-            scores = self.score.pop(unit) * scale + bias_t[:, 256 * tile:256 * tile + 256]
-            top = jnp.max(scores, axis=0, keepdims=True)
-            prob = jnp.exp(scores - top)
-            self.prob[unit] = prob.astype(BF16), jnp.sum(prob, axis=0, keepdims=True)
+            probs, totals = [], []
+            for half in range(2):
+                if unit in self.score:
+                    part = self.biased(unit, half)
+                    top = jnp.max(part, axis=0, keepdims=True)
+                else:
+                    part, top = part_sc[unit, half], top_sc[unit, half]
+                prob = jnp.exp2((part - top) * (SHRINK * LOG2_E))
+                totals.append(jnp.sum(prob, axis=0, keepdims=True))
+                probs.append(prob.astype(BF16))
+            self.prob[unit] = jnp.concatenate(probs, axis=1), jnp.concatenate(totals, axis=1)
 
         def mix(self, unit):
             slot, tile = self.slots[unit // 3], unit % 3
@@ -208,32 +251,26 @@
     def out_dot(sub, wo):
         return dot(gated_sc[sub].T, wo[...])
 
-    batch = 4
     loads[0].wait()
     for part in range(chunks):
         load_z(part).wait()
-
-        @pl.loop(0, chunk // batch)
-        def _(step):
-            base = chunk * part + step * batch
-            normed = [layer_norm(z_ref[base + sub]) for sub in range(batch)]
-            full = [dot(wb_s[...], duplicate_tail(val), 1, 1) for val in normed]
-            for sub in range(batch):
-                normed_sc[base + sub] = normed[sub]
-            for sub in range(batch):
-                row_bias[pl.ds(base + sub, 1), :] = bias_row(full[sub])
-
+        base = chunk * part
+        normed = [layer_norm(z_ref[base + sub]) for sub in range(chunk)]
+        full = [dot(wb_s[...], duplicate_tail(val), 1, 1) for val in normed]
+        for sub in range(chunk):
+            normed_sc[base + sub] = normed[sub]
+        for sub in range(chunk):
+            row_bias[base + sub:base + sub + 1, :] = bias_row(full[sub])
         publish_bias(0, part)
-        if part == 0:
+        if part == chunks - 2:
             loads[1].wait()
             transpose_weights(wp_s, wt_s)
             pl.semaphore_wait(barrier, group - 1)
-        if part == 1:
+            send_bias_part(0, 0, chunks - 1)
+        if part == chunks - 1:
             loads[2].wait()
             transpose_weights(wp_e, wt_e)
-        if part == 2:
-            stage(project(0, duplicate_tail(normed_sc[0]), wt_s, wp_s))
-        send_bias_part(0, part)
+            send_bias_part(0, chunks - 1)
 
     for load in loads[3:]:
         load.wait()
@@ -249,7 +286,7 @@
 
     wait_bias(0)
     low = low_half((64, 128))
-    by_query = jnp.concatenate([bias_of(0, src) for src in range(group)], axis=0)
+    by_query = jnp.concatenate([bias_of(0, src) for src in range(group)], axis=0) * (1 / SHRINK)
     by_query = jnp.concatenate([by_query, by_query[128:]], axis=0)
     for first in (0, 1):
         base = 384 * first
@@ -268,106 +305,152 @@
         row = 2 * pair + sub
         value = z_ref[row] + merge_tail(res)
         y_ref[row] = value
-        return value, duplicate_tail(layer_norm(value.astype(BF16).astype(F32)))
+        return value
 
     def store_h(pair, first, second):
         store_block(send_first, got_first, pair, first, second, 0, early)
-        store_block(send_rest, got_rest, pair, first, second, early, rows)
-
-    def start_tail(pair):
-        res = [out_dot(sub, wo_s) for sub in range(2)]
-        made = [start_resid(pair, sub, res[sub]) for sub in range(2)]
-        full = [dot(wb_e[...], made[sub][1], 1, 1) for sub in range(2)]
-        store_h(pair, made[0][0], made[1][0])
-        for sub in range(2):
-            row_bias[pl.ds(2 * pair + sub, 1), :] = bias_row(full[sub])
+        for idx in range(later):
+            for dest in range(group):
+                low = rows * dest + early * (idx + 1)
+                span = slice(low, low + early)
+                send_rest[dest, idx, pair] = jnp.concatenate([first[span], second[span]], axis=0).astype(BF16)
+            got_rest[me, idx, pair] = send_rest[me, idx, pair]
+
+    def end_normed(pair, sub):
+        return duplicate_tail(layer_norm(y_ref[2 * pair + sub].astype(BF16).astype(F32)))
+
+    def prime(slot):
+        att = Attention([slot])
+        for unit in range(2):
+            att.qk(unit)
+        for unit in range(2):
+            att.hand_on(unit)
+
+    prime(0)
 
     @pl.loop(0, pairs)
     def _(pair):
-        @pl.when(jnp.logical_and(pair > 2, lax.rem(pair, 2) == 1))
-        def _():
-            send_early(pair - 3, 2)
-
-        @pl.when(jnp.logical_and(pair > 4, lax.rem(pair, 2) == 1))
-        def _():
-            send_later(pair - 5, 2)
-
+        even = lax.rem(pair, 2) == 0
         for part in range(chunks - 1):
-            @pl.when(pair == (part + 1) * (chunk // 2) + 1)
+            @pl.when(pair == chunk // 2 * (part + 1) + 2)
             def _():
                 publish_bias(1, part)
 
-            @pl.when(pair == (part + 1) * (chunk // 2) + 2)
+        @pl.when(pair == 2)
+        def _():
+            send_early(0, 1)
+
+        @pl.when(jnp.logical_and(pair > 2, even))
+        def _():
+            send_early(pair - 3, 2)
+
+        @pl.when(pair == pairs - 1)
+        def _():
+            send_early(pairs - 3, 1)
+
+        @pl.when(pair == 4)
+        def _():
+            send_later(0, 1)
+
+        @pl.when(jnp.logical_and(jnp.logical_and(pair > 4, pair < held + 5), even))
+        def _():
+            send_later(pair - 5, 2)
+
+        for part in range(chunks - 1):
+            @pl.when(pair == chunk // 2 * (part + 1) + 2)
             def _():
                 send_bias_part(1, part)
 
         last = jnp.maximum(pair - 1, 0)
-        att = Attention([2 * pair, 2 * pair + 1])
-        att.qk(0)
-        res = [out_dot(sub, wo_s) for sub in range(2)]
-        att.qk(1)
+        older = jnp.maximum(pair - 2, 0)
+        att = Attention([2 * pair, 2 * pair + 1, 2 * jnp.minimum(pair + 1, pairs - 1)])
+        att.qk(2)
+        att.qk(3)
+        normed = [end_normed(older, sub) for sub in range(2)]
         att.soften(0)
         att.mix(0)
-        att.qk(2)
+        res = [out_dot(sub, wo_s) for sub in range(2)]
+        att.soften(1)
+        att.mix(1)
+        full = [dot(wb_e[...], val, 1, 1) for val in normed]
+        att.qk(4)
         made = [start_resid(last, 0, res[0])]
-        att.soften(1)
+        att.soften(2)
         att.norm(0)
-        att.mix(1)
-        att.qk(3)
+        att.mix(2)
+        att.qk(5)
         made.append(start_resid(last, 1, res[1]))
-        full = [dot(wb_e[...], made[0][1], 1, 1)]
-        att.soften(2)
+        att.soften(3)
         att.norm(1)
-        att.mix(2)
-        att.qk(4)
-        full.append(dot(wb_e[...], made[1][1], 1, 1))
-        store_h(last, made[0][0], made[1][0])
-        att.soften(3)
+        att.mix(3)
+        att.qk(6)
+        for sub in range(2):
+            row_bias[pl.ds(2 * older + sub, 1), :] = bias_row(full[sub])
+        att.soften(4)
         att.norm(2)
-        att.mix(3)
         att.gate(0)
-        att.qk(5)
-        row_bias[pl.ds(2 * last, 1), :] = bias_row(full[0])
-        att.soften(4)
+        att.mix(4)
+        att.qk(7)
+        att.soften(5)
         att.norm(3)
-        att.mix(4)
-        att.soften(5)
+        att.mix(5)
+        store_h(last, made[0], made[1])
+        att.hand_on(6)
         att.norm(4)
-        att.mix(5)
-        row_bias[pl.ds(2 * last + 1, 1), :] = bias_row(full[1])
+        att.hand_on(7)
         att.norm(5)
         att.gate(1)
 
-    start_tail(pairs - 1)
+    send_early(pairs - 2, 1)
+    res = [out_dot(sub, wo_s) for sub in range(2)]
+    made = [start_resid(pairs - 1, sub, res[sub]) for sub in range(2)]
+    store_h(pairs - 1, made[0], made[1])
+    ends = [(pair, sub) for pair in (pairs - 2, pairs - 1) for sub in range(2)]
+    full = [dot(wb_e[...], end_normed(pair, sub), 1, 1) for pair, sub in ends]
+    send_early(pairs - 1, 1)
+    for (pair, sub), val in zip(ends, full):
+        row_bias[2 * pair + sub:2 * pair + sub + 1, :] = bias_row(val)
     publish_bias(1, chunks - 1)
-    send_early(pairs - 2, 2)
+    send_last(0, held, pairs - held)
     send_bias_part(1, chunks - 1)
-    send_later(pairs - 4, 4)
-
-    def spread(got, low, high):
-        width = high - low
-
+    send_last(1, held, pairs - held)
+
+    def wait_blocks(view, recv_sem):
+        for peer in peers:
+            pltpu.make_async_copy(view(peer), view(peer), recv_sem.at[peer]).wait()
+
+    def spread(view, low, first, count):
         @pl.loop(0, group)
         def _(src):
-            @pl.loop(0, pairs)
-            def _(pair):
-                block = got[src, pair].astype(F32)
+            for pair in range(first, first + count):
+                block = view(src)[pair].astype(F32)
                 for sub in range(2):
                     start = pl.multiple_of(((src * pairs + pair) * 2 + sub) * rows + low, 8)
-                    flat[pl.ds(start, width), :] = block[width * sub:width * sub + width]
+                    flat[pl.ds(start, early), :] = block[early * sub:early * sub + early]
+
+    def spread_rest(idx):
+        if idx == 0:
+            wait_blocks(lambda src: got_rest.at[src, :, pl.ds(0, held)], rest_recv_sem.at[0])
+        wait_blocks(lambda src: got_rest.at[src, idx, pl.ds(held, pairs - held)], rest_recv_sem.at[1 + idx])
+        spread(lambda src: got_rest.at[src, idx], early * (idx + 1), 0, pairs)
 
     def column(col):
         return flat[pl.ds(col, seq_len, stride=rows), :]
 
-    wait_all(got_first, first_recv_sem)
-    spread(got_first, 0, early)
+    wait_blocks(lambda src: got_first.at[src, pl.ds(0, pairs - 1)], first_recv_sem.at[0])
+    spread(lambda src: got_first.at[src], 0, 0, pairs - 1)
+    wait_blocks(lambda src: got_first.at[src, pl.ds(pairs - 1, 1)], first_recv_sem.at[1])
+    spread(lambda src: got_first.at[src], 0, pairs - 1, 1)
+    forward_bias(1)
 
     for sub in range(2):
         stage(project(sub, duplicate_tail(layer_norm(column(sub))), wt_e, wp_e))
 
     wait_bias(1)
     for src in range(group):
-        bias_t[rows * src:rows * src + rows] = bias_of(1, src)
+        bias_t[rows * src:rows * src + rows] = bias_of(1, src) * (1 / SHRINK)
+
+    prime(0)
 
     def end_mid(pair, sub, res):
         upd = merge_tail(res)
@@ -385,63 +468,73 @@
 
     @pl.loop(0, pairs)
     def _(pair):
-        @pl.when(pair == early // 2 - 1)
-        def _():
-            wait_all(got_rest, rest_recv_sem)
-            spread(got_rest, early, rows)
-
-        @pl.when(pair > 1)
-        def _():
-            send_delta(pair - 2)
+        for idx in range(later):
+            @pl.when(pair == early // 2 * (idx + 1) - 1)
+            def _():
+                spread_rest(idx)
+
+        @pl.when(pair == 2)
+        def _():
+            send_delta(0, 1)
+
+        @pl.when(jnp.logical_and(pair > 2, lax.rem(pair, 2) == 0))
+        def _():
+            send_delta(pair - 3, 2)
+
+        @pl.when(pair == pairs - 1)
+        def _():
+            send_delta(pairs - 3, 1)
 
         last = jnp.maximum(pair - 1, 0)
         ahead = jnp.minimum(pair + 1, pairs - 1)
         here = 2 * lax.rem(pair, 2)
         there = 2 - here
-        att = Attention([here, here + 1])
-        att.qk(0)
-        res = [out_dot(sub, wo_e) for sub in range(2)]
-        att.qk(1)
+        att = Attention([here, here + 1, there])
+        att.qk(2)
+        att.qk(3)
         normed = [duplicate_tail(layer_norm(column(2 * ahead + sub))) for sub in range(2)]
         att.soften(0)
         att.mix(0)
+        res = [out_dot(sub, wo_e) for sub in range(2)]
+        att.soften(1)
+        att.mix(1)
         made = project(there, normed[0], wt_e, wp_e)
-        att.qk(2)
+        att.qk(4)
         mids = [end_mid(last, 0, res[0])]
-        att.soften(1)
+        att.soften(2)
         att.norm(0)
-        att.mix(1)
+        att.mix(2)
         stage(made)
-        att.qk(3)
+        att.qk(5)
         mids.append(end_mid(last, 1, res[1]))
         hidden = [widen(mids[0])]
-        att.soften(2)
+        att.soften(3)
         att.norm(1)
-        att.mix(2)
+        att.mix(3)
         hidden.append(widen(mids[1]))
-        att.qk(4)
+        att.qk(6)
         delta = [mids[0][0] + dot(hidden[0], w2_ref[...])]
-        att.soften(3)
+        att.soften(4)
         att.norm(2)
         att.gate(0)
-        att.mix(3)
+        att.mix(4)
+        made = project(there + 1, normed[1], wt_e, wp_e)
+        att.qk(7)
         delta.append(mids[1][0] + dot(hidden[1], w2_ref[...]))
-        att.qk(5)
-        made = project(there + 1, normed[1], wt_e, wp_e)
-        att.soften(4)
+        att.soften(5)
         att.norm(3)
-        att.mix(4)
+        att.mix(5)
         stage(made)
         store_block(send_d, got_d, last, delta[0], delta[1], 0, rows)
-        att.soften(5)
+        att.hand_on(6)
         att.norm(4)
-        att.mix(5)
+        att.hand_on(7)
         att.norm(5)
         att.gate(1)
 
-    send_delta(pairs - 2)
+    send_delta(pairs - 2, 1)
     end_tail(pairs - 1)
-    send_delta(pairs - 1)
+    send_delta(pairs - 1, 1)
 
     def finish(part, first, count):
         span = pl.ds(first, count)
@@ -450,8 +543,7 @@
 
         @pl.loop(0, group)
         def _(src):
-            @pl.loop(first, first + count)
-            def _(pair):
+            for pair in range(first, first + count):
                 start = pl.multiple_of((src * pairs + pair) * 2 * rows, 2 * rows)
                 flat[pl.ds(start, 2 * rows), :] = got_d[src, pair].astype(F32)
 
@@ -467,11 +559,16 @@
     def drain(ref, sem):
         pltpu.make_async_copy(ref, ref, sem).wait()
 
+    for phase in range(2):
+        for peer in peers if phase == 0 else alike + [partner]:
+            drain(send_bias.at[phase], bias_send_sem.at[phase, peer])
+    for src in alike:
+        drain(got_bias.at[1, src], pass_send_sem.at[src])
     for peer in peers:
-        for phase in range(2):
-            drain(send_bias.at[phase], bias_send_sem.at[phase, peer])
         drain(send_first.at[peer], first_send_sem.at[peer])
-        drain(send_rest.at[peer], rest_send_sem.at[peer])
+        drain(send_rest.at[peer, :, pl.ds(0, held)], rest_send_sem.at[0, peer])
+        for idx in range(later):
+            drain(send_rest.at[peer, idx, pl.ds(held, pairs - held)], rest_send_sem.at[1 + idx, peer])
         drain(send_d.at[peer], d_send_sem.at[peer])
 
 
@@ -487,6 +584,8 @@
         early = 8
         chunk = 8
         hbm = pl.BlockSpec(memory_space=pltpu.HBM)
+
+        later = pltpu.VMEM((group, rows // early - 1, pairs, 2 * early, channels), BF16)
 
         def exchange(width):
             return pltpu.VMEM((group, pairs, 2 * width, channels), BF16)
@@ -509,7 +608,9 @@
                 pltpu.VMEM((rows, channels, seq_len), BF16),
                 pltpu.VMEM((rows, channels, 256), F32),
                 pltpu.VMEM((2, channels, 256), BF16),
-                exchange(early), exchange(early), exchange(rows - early), exchange(rows - early), exchange(rows), exchange(rows),
+                pltpu.VMEM((2, 2, seq_len, 128), F32),
+                pltpu.VMEM((2, 2, 1, 128), F32),
+                exchange(early), exchange(early), later, later, exchange(rows), exchange(rows),
                 pltpu.VMEM((rows * seq_len, channels), F32),
                 pltpu.SemaphoreType.DMA((rows // chunk,)),
                 pltpu.SemaphoreType.DMA((8,)),
@@ -517,8 +618,9 @@
                 pltpu.SemaphoreType.DMA((2, group)),
                 pltpu.SemaphoreType.DMA((group,)),
                 pltpu.SemaphoreType.DMA((group,)),
-                pltpu.SemaphoreType.DMA((group,)),
-                pltpu.SemaphoreType.DMA((group,)),
+                pltpu.SemaphoreType.DMA((2, group)),
+                pltpu.SemaphoreType.DMA((rows // early, group)),
+                pltpu.SemaphoreType.DMA((rows // early, group)),
                 pltpu.SemaphoreType.DMA((group,)),
                 pltpu.SemaphoreType.DMA((2, group)),
             ],

time: 55.4 us -> 53.6 us (0.968)
  Pallas kernels: 53.6 us -> 52.1 us
    pallas_call x1, Pallas kernels: 53.6 us -> 52.1 us  [local_fn(): pl.pallas_call(functools.partial(kernel, 'sp', group, early), out_shape=j...]
where the time goes in v4:
time: 53.6 us; the launch traced here: 53.5 us
  Pallas kernels  52.1 us (97%)
  local copies, waits for them, and re-layouts  1.41 us (3%)
    pallas_call x1, Pallas kernels, local_fn(): pl.pallas_call(functools.partial(kernel, 'sp', group, early), out_shape=j...  52.1 us
    unnamed x1, local copies, waits for them, and re-layouts  1.41 us

profile of v4, /device:TPU:112, one launch (start us, length us, event | category | flops | bytes accessed | tf_op | source)
XLA Modules:
  0.0 53.5 jit_solution(17224121239103989614)
XLA Ops:
  0.0 52.1 %shard_map.91 = f32[24,192,128]{2,1,0:T(8,128)S(1)} custom-call(f32[24,192,128]{2,1,0:T(8,128)} %z_hbm.1, bf16[128,512]{1,0:T(8,128)(2,1)} %wp_s_hbm.1, bf16[4,128]{1,0:T(4,128)(2,1)} %wb_s_hbm.1, bf16[128,128]{1,0:T(8,128)(2,1)} %wo_s_hbm.1, bf16[128,512]{1,0:T(8,128)(2,1)} %wp_e_hbm.1, bf16[4,128]{1,0:T(4,128)(2,1)} %wb_e_hbm.1, ...), custom_call_target="tpu_custom_call" | custom-call | tf_op jit(solution)/shard_map/pallas_call | solution.py:593
  52.1 1.4 %copy.11 = f32[24,192,128]{2,1,0:T(8,128)} copy(f32[24,192,128]{2,1,0:T(8,128)S(1)} %shard_map.91) | data formatting | bytes 4718592

commit v5 on v4

--- a/solution.py
+++ b/solution.py
@@ -8,6 +8,10 @@
 from jax.sharding import PartitionSpec as P
 
 LN_EPS = 1e-5
+LANES = 128
+DOUBLE = 256
+HALF = 64
+HEAD = 32
 Q_SHRINK = 0.125
 SHRINK = 32 ** -0.5 / Q_SHRINK
 LOG2_E = 1.4426950408889634
@@ -28,19 +32,19 @@
 
 
 def duplicate_tail(normed):
-    return jnp.concatenate([normed, normed[128:]], axis=0)
+    return jnp.concatenate([normed, normed[LANES:]], axis=0)
 
 
 def low_half(shape):
-    return lax.broadcasted_iota(jnp.int32, shape, len(shape) - 1) < 64
+    return lax.broadcasted_iota(jnp.int32, shape, len(shape) - 1) < HALF
 
 
 def bias_row(full):
-    low = low_half((1, 128))
+    low = low_half((1, LANES))
     tiles = []
     for first in (0, 2):
         head_a, head_b = full[first:first + 1], full[first + 1:first + 2]
-        tiles += [head_a[:, :128], jnp.where(low, head_a[:, 128:], head_b[:, 128:]), head_b[:, :128]]
+        tiles += [head_a[:, :LANES], jnp.where(low, head_a[:, LANES:], head_b[:, LANES:]), head_b[:, :LANES]]
     return jnp.concatenate(tiles, axis=1)
 
 
@@ -57,11 +61,11 @@
 
 
 def score_block(q_t, tile):
-    zero = jnp.zeros((32, 128), BF16)
+    zero = jnp.zeros((HEAD, LANES), BF16)
     none = [zero, zero]
 
     def head(idx):
-        return q_t[32 * idx:32 * idx + 32, :128], q_t[32 * idx:32 * idx + 32, 128:]
+        return q_t[HEAD * idx:HEAD * idx + HEAD, :LANES], q_t[HEAD * idx:HEAD * idx + HEAD, LANES:]
 
     first, second = head(tile), head(tile + 1)
     if tile == 0:
@@ -72,28 +76,27 @@
 
 
 def gather_heads(outs, g_t):
-    main = jnp.concatenate([outs[0][:32, :128], outs[1][:32, :128], outs[1][32:, 128:], outs[2][32:, 128:]], axis=0)
-    tail = jnp.concatenate([keep_low(outs[0][:32, 128:]), keep_high(outs[0][32:, 128:]),
-                            keep_low(outs[2][:32, :128]), keep_high(outs[2][32:, :128])], axis=0)
+    main = jnp.concatenate([outs[0][:HEAD, :LANES], outs[1][:HEAD, :LANES], outs[1][HEAD:, LANES:], outs[2][HEAD:, LANES:]], axis=0)
+    tail = jnp.concatenate([keep_low(outs[0][:HEAD, LANES:]), keep_high(outs[0][HEAD:, LANES:]),
+                            keep_low(outs[2][:HEAD, :LANES]), keep_high(outs[2][HEAD:, :LANES])], axis=0)
     return (jnp.concatenate([main, tail], axis=1) * g_t).astype(BF16)
 
 
 def merge_tail(res):
-    return jnp.concatenate([res[:128], res[128:192] + res[192:]], axis=0)
+    return jnp.concatenate([res[:LANES], res[LANES:192] + res[192:]], axis=0)
 
 
 def kernel(axis, group, early, z_hbm, wp_s_hbm, wb_s_hbm, wo_s_hbm, wp_e_hbm, wb_e_hbm, wo_e_hbm, w1_hbm, w2_hbm, y_ref,
            z_ref, wp_s, wb_s, wo_s, wp_e, wb_e, wo_e, w1_ref, w2_ref,
            wt_s, wt_e, row_bias, send_bias, got_bias, bias_t, normed_sc, q_sc, k_sc, v_sc, g_sc, gated_sc, part_sc, top_sc,
-           send_first, got_first, send_rest, got_rest, send_d, got_d, flat,
-           z_sem, w_sem, bias_send_sem, bias_recv_sem, pass_send_sem, first_send_sem, first_recv_sem, rest_send_sem, rest_recv_sem,
-           d_send_sem, d_recv_sem):
+           send_h, got_h, send_d, got_d, flat,
+           z_sem, w_sem, bias_send_sem, bias_recv_sem, pass_send_sem, h_send_sem, h_recv_sem, d_send_sem, d_recv_sem):
     rows, seq_len, channels = z_hbm.shape
     pairs = rows // 2
     chunk = 8
     chunks = rows // chunk
     late = pairs - 3
-    later = rows // early - 1
+    groups = rows // early
     held = pairs - 7
     me = lax.axis_index(axis)
     half = group // 2
@@ -122,33 +125,32 @@
     for load in loads[2:]:
         load.start()
 
-    def send_bias_part(phase, part, count=1):
+    def send_bias_part(phase, part, count, to, sem):
         span = pl.ds(part, count)
-        for peer in peers if phase == 0 else alike + [partner]:
+        for peer in to:
             pltpu.make_async_remote_copy(
                 src_ref=send_bias.at[phase, span], dst_ref=got_bias.at[phase, me, span],
-                send_sem=bias_send_sem.at[phase, peer], recv_sem=bias_recv_sem.at[phase, me],
+                send_sem=bias_send_sem.at[sem, peer], recv_sem=bias_recv_sem.at[sem, me],
                 device_id={axis: peer}, device_id_type=MESH).start()
 
-    def wait_for_bias(phase, src):
-        pltpu.make_async_copy(got_bias.at[phase, src], got_bias.at[phase, src], bias_recv_sem.at[phase, src]).wait()
-
-    def forward_bias(phase):
+    def drain(ref, sem):
+        pltpu.make_async_copy(ref, ref, sem).wait()
+
+    most, final = pl.ds(0, chunks - 1), pl.ds(chunks - 1, 1)
+
+    def forward_bias():
         for src in alike:
-            wait_for_bias(phase, src)
+            view = got_bias.at[1, src, most]
+            drain(view, bias_recv_sem.at[1, src])
             pltpu.make_async_remote_copy(
-                src_ref=got_bias.at[phase, src], dst_ref=got_bias.at[phase, src],
-                send_sem=pass_send_sem.at[src], recv_sem=bias_recv_sem.at[phase, src],
+                src_ref=view, dst_ref=view,
+                send_sem=pass_send_sem.at[src], recv_sem=bias_recv_sem.at[1, src],
                 device_id={axis: partner}, device_id_type=MESH).start()
 
     def publish_bias(phase, part):
         rounded = row_bias[chunk * part:chunk * part + chunk].astype(BF16)
         send_bias[phase, part] = rounded
         got_bias[phase, me, part] = rounded
-
-    def wait_bias(phase):
-        for src in peers if phase == 0 else [partner] + others:
-            wait_for_bias(phase, src)
 
     def send_blocks(send, got, send_sem, recv_sem, start, count):
         span = pl.ds(start, count)
@@ -158,24 +160,30 @@
                 send_sem=send_sem.at[peer], recv_sem=recv_sem.at[me],
                 device_id={axis: peer}, device_id_type=MESH).start()
 
-    def send_early(start, count):
-        send_blocks(send_first, got_first, first_send_sem, first_recv_sem.at[int(isinstance(start, int) and start == pairs - 1)], start, count)
-
-    def send_later(start, count):
-        span = pl.ds(start, count)
+    def send_h_view(sem, view):
         for peer in peers:
             pltpu.make_async_remote_copy(
-                src_ref=send_rest.at[peer, :, span], dst_ref=got_rest.at[me, :, span],
-                send_sem=rest_send_sem.at[0, peer], recv_sem=rest_recv_sem.at[0, me],
+                src_ref=view(send_h, peer), dst_ref=view(got_h, me),
+                send_sem=h_send_sem.at[sem, peer], recv_sem=h_recv_sem.at[sem, me],
                 device_id={axis: peer}, device_id_type=MESH).start()
 
-    def send_last(idx, start, count):
-        span = pl.ds(start, count)
+    def wide_view(start, count):
+        return lambda ref, who: ref.at[who, :, pl.ds(start, count)]
+
+    def group_view(idx, start, count):
+        return lambda ref, who: ref.at[who, idx, pl.ds(start, count)]
+
+    WIDE, FIRST, LAST = range(3)
+    whole_views = [wide_view(0, held), group_view(0, held, pairs - 1 - held), group_view(0, pairs - 1, 1)]
+    whole_views += [group_view(idx, held, pairs - held) for idx in range(1, groups)]
+
+    def wait_h(sem):
         for peer in peers:
-            pltpu.make_async_remote_copy(
-                src_ref=send_rest.at[peer, idx, span], dst_ref=got_rest.at[me, idx, span],
-                send_sem=rest_send_sem.at[1 + idx, peer], recv_sem=rest_recv_sem.at[1 + idx, me],
-                device_id={axis: peer}, device_id_type=MESH).start()
+            view = whole_views[sem](got_h, peer)
+            pltpu.make_async_copy(view, view, h_recv_sem.at[sem, peer]).wait()
+
+    def send_first(start, count):
+        send_h_view(FIRST, group_view(0, start, count))
 
     def send_delta(start, count):
         send_blocks(send_d, got_d, d_send_sem, d_recv_sem.at[start // late], start, count)
@@ -213,8 +221,8 @@
             self.score[unit] = dot(k_sc[slot], score_block(q_sc[slot], tile))
 
         def biased(self, unit, half):
-            at = 256 * (unit % 3) + 128 * half
-            return self.score[unit][:, 128 * half:128 * half + 128] + bias_t[:, at:at + 128]
+            at = DOUBLE * (unit % 3) + LANES * half
+            return self.score[unit][:, LANES * half:LANES * half + LANES] + bias_t[:, at:at + LANES]
 
         def hand_on(self, unit):
             for half in range(2):
@@ -238,7 +246,7 @@
         def mix(self, unit):
             slot, tile = self.slots[unit // 3], unit % 3
             prob, total = self.prob.pop(unit)
-            self.mixed[unit] = dot(v_sc[slot, 32 * tile:32 * tile + 64], prob), total
+            self.mixed[unit] = dot(v_sc[slot, HEAD * tile:HEAD * tile + HALF], prob), total
 
         def norm(self, unit):
             mixed, total = self.mixed.pop(unit)
@@ -266,14 +274,11 @@
             loads[1].wait()
             transpose_weights(wp_s, wt_s)
             pl.semaphore_wait(barrier, group - 1)
-            send_bias_part(0, 0, chunks - 1)
-        if part == chunks - 1:
-            loads[2].wait()
-            transpose_weights(wp_e, wt_e)
-            send_bias_part(0, chunks - 1)
+            send_bias_part(0, 0, chunks - 1, peers, 0)
 
     for load in loads[3:]:
         load.wait()
+    send_bias_part(0, chunks - 1, 1, peers, 0)
 
     @pl.loop(0, pairs)
     def _(step):
@@ -284,22 +289,25 @@
     def bias_of(phase, src):
         return jnp.concatenate([got_bias[phase, src, part].astype(F32) for part in range(chunks)], axis=0)
 
-    wait_bias(0)
-    low = low_half((64, 128))
+    loads[2].wait()
+    transpose_weights(wp_e, wt_e)
+    for src in peers:
+        drain(got_bias.at[0, src], bias_recv_sem.at[0, src])
+    low = low_half((HALF, LANES))
     by_query = jnp.concatenate([bias_of(0, src) for src in range(group)], axis=0) * (1 / SHRINK)
-    by_query = jnp.concatenate([by_query, by_query[128:]], axis=0)
+    by_query = jnp.concatenate([by_query, by_query[LANES:]], axis=0)
     for first in (0, 1):
         base = 384 * first
-        head_a = by_query[:, base:base + 128].T
-        mixed = by_query[:, base + 128:base + 256].T
-        head_b = by_query[:, base + 256:base + 384].T
-        bias_t[0:128, base:base + 128] = head_a[:, :128]
-        bias_t[128:192, base:base + 128] = mixed[:64, :128]
-        low_a = low_half((128, 128))
-        bias_t[0:128, base + 128:base + 256] = jnp.where(low_a, head_a[:, 128:], head_b[:, 128:])
-        bias_t[128:192, base + 128:base + 256] = jnp.where(low, mixed[:64, 128:], mixed[64:, 128:])
-        bias_t[0:128, base + 256:base + 384] = head_b[:, :128]
-        bias_t[128:192, base + 256:base + 384] = mixed[64:, :128]
+        head_a = by_query[:, base:base + LANES].T
+        mixed = by_query[:, base + LANES:base + DOUBLE].T
+        head_b = by_query[:, base + DOUBLE:base + 384].T
+        bias_t[0:LANES, base:base + LANES] = head_a[:, :LANES]
+        bias_t[LANES:192, base:base + LANES] = mixed[:HALF, :LANES]
+        low_a = low_half((LANES, LANES))
+        bias_t[0:LANES, base + LANES:base + DOUBLE] = jnp.where(low_a, head_a[:, LANES:], head_b[:, LANES:])
+        bias_t[LANES:192, base + LANES:base + DOUBLE] = jnp.where(low, mixed[:HALF, LANES:], mixed[HALF:, LANES:])
+        bias_t[0:LANES, base + DOUBLE:base + 384] = head_b[:, :LANES]
+        bias_t[LANES:192, base + DOUBLE:base + 384] = mixed[HALF:, :LANES]
 
     def start_resid(pair, sub, res):
         row = 2 * pair + sub
@@ -308,13 +316,12 @@
         return value
 
     def store_h(pair, first, second):
-        store_block(send_first, got_first, pair, first, second, 0, early)
-        for idx in range(later):
+        for idx in range(groups):
             for dest in range(group):
-                low = rows * dest + early * (idx + 1)
+                low = rows * dest + early * idx
                 span = slice(low, low + early)
-                send_rest[dest, idx, pair] = jnp.concatenate([first[span], second[span]], axis=0).astype(BF16)
-            got_rest[me, idx, pair] = send_rest[me, idx, pair]
+                send_h[dest, idx, pair] = jnp.concatenate([first[span], second[span]], axis=0).astype(BF16)
+            got_h[me, idx, pair] = send_h[me, idx, pair]
 
     def end_normed(pair, sub):
         return duplicate_tail(layer_norm(y_ref[2 * pair + sub].astype(BF16).astype(F32)))
@@ -338,28 +345,24 @@
 
         @pl.when(pair == 2)
         def _():
-            send_early(0, 1)
-
-        @pl.when(jnp.logical_and(pair > 2, even))
+            send_h_view(WIDE, wide_view(0, 1))
+
+        @pl.when(jnp.logical_and(jnp.logical_and(pair > 2, pair < held + 2), even))
         def _():
-            send_early(pair - 3, 2)
+            send_h_view(WIDE, wide_view(pair - 3, 2))
+
+        @pl.when(jnp.logical_and(pair > held + 2, even))
+        def _():
+            send_first(pair - 3, 2)
 
         @pl.when(pair == pairs - 1)
         def _():
-            send_early(pairs - 3, 1)
-
-        @pl.when(pair == 4)
-        def _():
-            send_later(0, 1)
-
-        @pl.when(jnp.logical_and(jnp.logical_and(pair > 4, pair < held + 5), even))
-        def _():
-            send_later(pair - 5, 2)
+            send_first(pairs - 3, 1)
 
         for part in range(chunks - 1):
             @pl.when(pair == chunk // 2 * (part + 1) + 2)
             def _():
-                send_bias_part(1, part)
+                send_bias_part(1, part, 1, alike + [partner], 1)
 
         last = jnp.maximum(pair - 1, 0)
         older = jnp.maximum(pair - 2, 0)
@@ -401,52 +404,48 @@
         att.norm(5)
         att.gate(1)
 
-    send_early(pairs - 2, 1)
+    send_first(pairs - 2, 1)
     res = [out_dot(sub, wo_s) for sub in range(2)]
     made = [start_resid(pairs - 1, sub, res[sub]) for sub in range(2)]
     store_h(pairs - 1, made[0], made[1])
     ends = [(pair, sub) for pair in (pairs - 2, pairs - 1) for sub in range(2)]
     full = [dot(wb_e[...], end_normed(pair, sub), 1, 1) for pair, sub in ends]
-    send_early(pairs - 1, 1)
+    send_h_view(LAST, group_view(0, pairs - 1, 1))
     for (pair, sub), val in zip(ends, full):
         row_bias[2 * pair + sub:2 * pair + sub + 1, :] = bias_row(val)
     publish_bias(1, chunks - 1)
-    send_last(0, held, pairs - held)
-    send_bias_part(1, chunks - 1)
-    send_last(1, held, pairs - held)
-
-    def wait_blocks(view, recv_sem):
-        for peer in peers:
-            pltpu.make_async_copy(view(peer), view(peer), recv_sem.at[peer]).wait()
-
-    def spread(view, low, first, count):
+    for peer in peers:
+        drain(send_bias.at[0], bias_send_sem.at[0, peer])
+    send_bias_part(1, chunks - 1, 1, peers, 2)
+    for idx in range(1, groups):
+        send_h_view(LAST + idx, group_view(idx, held, pairs - held))
+
+    def spread(idx, first, count):
         @pl.loop(0, group)
         def _(src):
             for pair in range(first, first + count):
-                block = view(src)[pair].astype(F32)
+                block = got_h[src, idx, pair].astype(F32)
                 for sub in range(2):
-                    start = pl.multiple_of(((src * pairs + pair) * 2 + sub) * rows + low, 8)
+                    start = pl.multiple_of(((src * pairs + pair) * 2 + sub) * rows + early * idx, 8)
                     flat[pl.ds(start, early), :] = block[early * sub:early * sub + early]
-
-    def spread_rest(idx):
-        if idx == 0:
-            wait_blocks(lambda src: got_rest.at[src, :, pl.ds(0, held)], rest_recv_sem.at[0])
-        wait_blocks(lambda src: got_rest.at[src, idx, pl.ds(held, pairs - held)], rest_recv_sem.at[1 + idx])
-        spread(lambda src: got_rest.at[src, idx], early * (idx + 1), 0, pairs)
 
     def column(col):
         return flat[pl.ds(col, seq_len, stride=rows), :]
 
-    wait_blocks(lambda src: got_first.at[src, pl.ds(0, pairs - 1)], first_recv_sem.at[0])
-    spread(lambda src: got_first.at[src], 0, 0, pairs - 1)
-    wait_blocks(lambda src: got_first.at[src, pl.ds(pairs - 1, 1)], first_recv_sem.at[1])
-    spread(lambda src: got_first.at[src], 0, pairs - 1, 1)
-    forward_bias(1)
+    wait_h(WIDE)
+    wait_h(FIRST)
+    spread(0, 0, pairs - 1)
+    wait_h(LAST)
+    spread(0, pairs - 1, 1)
+    forward_bias()
 
     for sub in range(2):
         stage(project(sub, duplicate_tail(layer_norm(column(sub))), wt_e, wp_e))
 
-    wait_bias(1)
+    for src in [partner] + others:
+        drain(got_bias.at[1, src, most], bias_recv_sem.at[1, src])
+    for src in peers:
+        drain(got_bias.at[1, src, final], bias_recv_sem.at[2, src])
     for src in range(group):
         bias_t[rows * src:rows * src + rows] = bias_of(1, src) * (1 / SHRINK)
 
@@ -457,7 +456,7 @@
         return upd, layer_norm(column(2 * pair + sub) + upd)
 
     def widen(mid):
-        return jnp.maximum(dot(mid[1], w1_ref[...]), 0.0).astype(BF16)
+        return jnp.maximum(dot(mid[1], w1_ref[...]).astype(BF16), jnp.asarray(0, BF16))
 
     def end_tail(pair):
         res = [out_dot(sub, wo_e) for sub in range(2)]
@@ -468,10 +467,11 @@
 
     @pl.loop(0, pairs)
     def _(pair):
-        for idx in range(later):
-            @pl.when(pair == early // 2 * (idx + 1) - 1)
+        for idx in range(1, groups):
+            @pl.when(pair == early // 2 * idx - 1)
             def _():
-                spread_rest(idx)
+                wait_h(LAST + idx)
+                spread(idx, 0, pairs)
 
         @pl.when(pair == 2)
         def _():
@@ -556,19 +556,14 @@
     finish(0, 0, late)
     finish(1, late, pairs - late)
 
-    def drain(ref, sem):
-        pltpu.make_async_copy(ref, ref, sem).wait()
-
-    for phase in range(2):
-        for peer in peers if phase == 0 else alike + [partner]:
-            drain(send_bias.at[phase], bias_send_sem.at[phase, peer])
+    for peer in alike + [partner]:
+        drain(send_bias.at[1, most], bias_send_sem.at[1, peer])
     for src in alike:
-        drain(got_bias.at[1, src], pass_send_sem.at[src])
+        drain(got_bias.at[1, src, most], pass_send_sem.at[src])
     for peer in peers:
-        drain(send_first.at[peer], first_send_sem.at[peer])
-        drain(send_rest.at[peer, :, pl.ds(0, held)], rest_send_sem.at[0, peer])
-        for idx in range(later):
-            drain(send_rest.at[peer, idx, pl.ds(held, pairs - held)], rest_send_sem.at[1 + idx, peer])
+        drain(send_bias.at[1, final], bias_send_sem.at[2, peer])
+        for sem, view in enumerate(whole_views):
+            drain(view(send_h, peer), h_send_sem.at[sem, peer])
         drain(send_d.at[peer], d_send_sem.at[peer])
 
 
@@ -585,10 +580,12 @@
         chunk = 8
         hbm = pl.BlockSpec(memory_space=pltpu.HBM)
 
-        later = pltpu.VMEM((group, rows // early - 1, pairs, 2 * early, channels), BF16)
-
-        def exchange(width):
-            return pltpu.VMEM((group, pairs, 2 * width, channels), BF16)
+        groups = rows // early
+        columns = pltpu.VMEM((group, groups, pairs, 2 * early, channels), BF16)
+        deltas = pltpu.VMEM((group, pairs, 2 * rows, channels), BF16)
+
+        def sems(*shape):
+            return pltpu.SemaphoreType.DMA(shape)
 
         return pl.pallas_call(
             functools.partial(kernel, 'sp', group, early),
@@ -603,26 +600,17 @@
                 pltpu.VMEM((2, group, rows // chunk, chunk, wide), BF16),
                 pltpu.VMEM((seq_len, wide), F32),
                 pltpu.VMEM((rows, seq_len, channels), BF16),
-                pltpu.VMEM((rows, channels, 256), BF16),
+                pltpu.VMEM((rows, channels, DOUBLE), BF16),
                 pltpu.VMEM((rows, seq_len, channels), BF16),
                 pltpu.VMEM((rows, channels, seq_len), BF16),
-                pltpu.VMEM((rows, channels, 256), F32),
-                pltpu.VMEM((2, channels, 256), BF16),
-                pltpu.VMEM((2, 2, seq_len, 128), F32),
-                pltpu.VMEM((2, 2, 1, 128), F32),
-                exchange(early), exchange(early), later, later, exchange(rows), exchange(rows),
+                pltpu.VMEM((rows, channels, DOUBLE), F32),
+                pltpu.VMEM((2, channels, DOUBLE), BF16),
+                pltpu.VMEM((2, 2, seq_len, LANES), F32),
+                pltpu.VMEM((2, 2, 1, LANES), F32),
+                columns, columns, deltas, deltas,
                 pltpu.VMEM((rows * seq_len, channels), F32),
-                pltpu.SemaphoreType.DMA((rows // chunk,)),
-                pltpu.SemaphoreType.DMA((8,)),
-                pltpu.SemaphoreType.DMA((2, group)),
-                pltpu.SemaphoreType.DMA((2, group)),
-                pltpu.SemaphoreType.DMA((group,)),
-                pltpu.SemaphoreType.DMA((group,)),
-                pltpu.SemaphoreType.DMA((2, group)),
-                pltpu.SemaphoreType.DMA((rows // early, group)),
-                pltpu.SemaphoreType.DMA((rows // early, group)),
-                pltpu.SemaphoreType.DMA((group,)),
-                pltpu.SemaphoreType.DMA((2, group)),
+                sems(rows // chunk), sems(len(weights)), sems(3, group), sems(3, group), sems(group),
+                sems(groups + 2, group), sems(groups + 2, group), sems(group), sems(2, group),
             ],
             compiler_params=pltpu.CompilerParams(collective_id=0, has_side_effects=True, vmem_limit_bytes=34 * 1024 * 1024),
         )(*[pltpu.with_memory_space_constraint(val, pltpu.HBM) for val in (pair_loc, *weights)])

time: 53.6 us -> 50.1 us (0.935)
  Pallas kernels: 52.1 us -> 48.6 us
    pallas_call x1, Pallas kernels: 52.1 us -> 48.6 us  [local_fn(): pl.pallas_call(functools.partial(kernel, 'sp', group, early), out_shape=j...]
where the time goes in v5:
time: 50.1 us; the launch traced here: 50 us
  Pallas kernels  48.6 us (97%)
  local copies, waits for them, and re-layouts  1.41 us (3%)
    pallas_call x1, Pallas kernels, local_fn(): pl.pallas_call(functools.partial(kernel, 'sp', group, early), out_shape=j...  48.6 us
    unnamed x1, local copies, waits for them, and re-layouts  1.41 us

profile of v5, /device:TPU:112, one launch (start us, length us, event | category | flops | bytes accessed | tf_op | source)
XLA Modules:
  0.0 50.0 jit_solution(6870596946019707211)
XLA Ops:
  0.0 48.6 %shard_map.91 = f32[24,192,128]{2,1,0:T(8,128)S(1)} custom-call(f32[24,192,128]{2,1,0:T(8,128)} %z_hbm.1, bf16[128,512]{1,0:T(8,128)(2,1)} %wp_s_hbm.1, bf16[4,128]{1,0:T(4,128)(2,1)} %wb_s_hbm.1, bf16[128,128]{1,0:T(8,128)(2,1)} %wo_s_hbm.1, bf16[128,512]{1,0:T(8,128)(2,1)} %wp_e_hbm.1, bf16[4,128]{1,0:T(4,128)(2,1)} %wb_e_hbm.1, ...), custom_call_target="tpu_custom_call" | custom-call | tf_op jit(solution)/shard_map/pallas_call | solution.py:590
  48.6 1.4 %copy.11 = f32[24,192,128]{2,1,0:T(8,128)} copy(f32[24,192,128]{2,1,0:T(8,128)S(1)} %shard_map.91) | data formatting | bytes 4718592

commit v6 on v5

--- a/solution.py
+++ b/solution.py
@@ -97,7 +97,7 @@
     chunks = rows // chunk
     late = pairs - 3
     groups = rows // early
-    held = pairs - 7
+    held = pairs - 9
     me = lax.axis_index(axis)
     half = group // 2
     order = sorted(range(1, group), key=lambda step: abs(step - half))
@@ -106,24 +106,22 @@
     alike = [lax.rem(me + step, group) for step in order if step % 2 == 0]
     others = [lax.rem(partner + step, group) for step in order if step % 2 == 0]
 
+    def load_z(idx):
+        span = pl.ds(idx * chunk, chunk)
+        return pltpu.make_async_copy(z_hbm.at[span], z_ref.at[span], z_sem.at[idx])
+
+    loads = [pltpu.make_async_copy(src, dst, w_sem.at[idx]) for idx, (src, dst) in enumerate(
+        ((wb_s_hbm, wb_s), (wp_s_hbm, wp_s), (wp_e_hbm, wp_e), (wo_s_hbm, wo_s), (wb_e_hbm, wb_e),
+         (wo_e_hbm, wo_e), (w1_hbm, w1_ref), (w2_hbm, w2_ref)))]
+    loads[0].start()
+    for idx in range(chunks):
+        load_z(idx).start()
+    for load in loads[1:]:
+        load.start()
+
     barrier = pltpu.get_barrier_semaphore()
     for peer in peers:
         pl.semaphore_signal(barrier, inc=1, device_id={axis: peer}, device_id_type=MESH)
-
-    def load_z(idx):
-        span = pl.ds(idx * chunk, chunk)
-        return pltpu.make_async_copy(z_hbm.at[span], z_ref.at[span], z_sem.at[idx])
-
-    loads = [pltpu.make_async_copy(src, dst, w_sem.at[idx]) for idx, (src, dst) in enumerate(
-        ((wb_s_hbm, wb_s), (wp_s_hbm, wp_s), (wp_e_hbm, wp_e), (wo_s_hbm, wo_s), (wb_e_hbm, wb_e),
-         (wo_e_hbm, wo_e), (w1_hbm, w1_ref), (w2_hbm, w2_ref)))]
-    load_z(0).start()
-    loads[0].start()
-    loads[1].start()
-    for idx in range(1, chunks):
-        load_z(idx).start()
-    for load in loads[2:]:
-        load.start()
 
     def send_bias_part(phase, part, count, to, sem):
         span = pl.ds(part, count)
@@ -271,14 +269,13 @@
             row_bias[base + sub:base + sub + 1, :] = bias_row(full[sub])
         publish_bias(0, part)
         if part == chunks - 2:
-            loads[1].wait()
-            transpose_weights(wp_s, wt_s)
             pl.semaphore_wait(barrier, group - 1)
             send_bias_part(0, 0, chunks - 1, peers, 0)
 
-    for load in loads[3:]:
+    for load in loads[1:]:
         load.wait()
     send_bias_part(0, chunks - 1, 1, peers, 0)
+    transpose_weights(wp_s, wt_s)
 
     @pl.loop(0, pairs)
     def _(step):
@@ -289,7 +286,6 @@
     def bias_of(phase, src):
         return jnp.concatenate([got_bias[phase, src, part].astype(F32) for part in range(chunks)], axis=0)
 
-    loads[2].wait()
     transpose_weights(wp_e, wt_e)
     for src in peers:
         drain(got_bias.at[0, src], bias_recv_sem.at[0, src])
@@ -367,41 +363,44 @@
         last = jnp.maximum(pair - 1, 0)
         older = jnp.maximum(pair - 2, 0)
         att = Attention([2 * pair, 2 * pair + 1, 2 * jnp.minimum(pair + 1, pairs - 1)])
+        normed0 = end_normed(older, 0)
+        att.qk(3)
+        normed1 = end_normed(older, 1)
+        att.soften(0)
+        res1 = out_dot(1, wo_s)
         att.qk(2)
-        att.qk(3)
-        normed = [end_normed(older, sub) for sub in range(2)]
-        att.soften(0)
         att.mix(0)
-        res = [out_dot(sub, wo_s) for sub in range(2)]
         att.soften(1)
+        att.soften(2)
+        res0 = out_dot(0, wo_s)
         att.mix(1)
-        full = [dot(wb_e[...], val, 1, 1) for val in normed]
+        made0 = start_resid(last, 0, res0)
+        full1 = dot(wb_e[...], normed1, 1, 1)
         att.qk(4)
-        made = [start_resid(last, 0, res[0])]
-        att.soften(2)
+        full0 = dot(wb_e[...], normed0, 1, 1)
+        att.norm(1)
+        att.soften(3)
+        att.mix(2)
         att.norm(0)
-        att.mix(2)
         att.qk(5)
-        made.append(start_resid(last, 1, res[1]))
-        att.soften(3)
-        att.norm(1)
-        att.mix(3)
+        made1 = start_resid(last, 1, res1)
+        att.soften(5)
+        att.soften(4)
         att.qk(6)
-        for sub in range(2):
-            row_bias[pl.ds(2 * older + sub, 1), :] = bias_row(full[sub])
-        att.soften(4)
         att.norm(2)
         att.gate(0)
+        att.qk(7)
+        att.mix(3)
         att.mix(4)
-        att.qk(7)
-        att.soften(5)
+        att.mix(5)
+        store_h(last, made0, made1)
+        row_bias[pl.ds(2 * older, 1), :] = bias_row(full0)
+        att.norm(4)
+        att.norm(5)
+        att.hand_on(6)
+        row_bias[pl.ds(2 * older + 1, 1), :] = bias_row(full1)
         att.norm(3)
-        att.mix(5)
-        store_h(last, made[0], made[1])
-        att.hand_on(6)
-        att.norm(4)
         att.hand_on(7)
-        att.norm(5)
         att.gate(1)
 
     send_first(pairs - 2, 1)
@@ -409,8 +408,8 @@
     made = [start_resid(pairs - 1, sub, res[sub]) for sub in range(2)]
     store_h(pairs - 1, made[0], made[1])
     ends = [(pair, sub) for pair in (pairs - 2, pairs - 1) for sub in range(2)]
+    send_h_view(LAST, group_view(0, pairs - 1, 1))
     full = [dot(wb_e[...], end_normed(pair, sub), 1, 1) for pair, sub in ends]
-    send_h_view(LAST, group_view(0, pairs - 1, 1))
     for (pair, sub), val in zip(ends, full):
         row_bias[2 * pair + sub:2 * pair + sub + 1, :] = bias_row(val)
     publish_bias(1, chunks - 1)
@@ -490,46 +489,48 @@
         here = 2 * lax.rem(pair, 2)
         there = 2 - here
         att = Attention([here, here + 1, there])
+        normed1 = duplicate_tail(layer_norm(column(2 * ahead + 1)))
         att.qk(2)
         att.qk(3)
-        normed = [duplicate_tail(layer_norm(column(2 * ahead + sub))) for sub in range(2)]
         att.soften(0)
+        res0 = out_dot(0, wo_e)
+        res1 = out_dot(1, wo_e)
+        att.soften(1)
+        normed0 = duplicate_tail(layer_norm(column(2 * ahead)))
+        att.mix(1)
+        next0 = project(there, normed0, wt_e, wp_e)
+        mid0 = end_mid(last, 0, res0)
+        att.norm(1)
+        att.soften(2)
         att.mix(0)
-        res = [out_dot(sub, wo_e) for sub in range(2)]
-        att.soften(1)
-        att.mix(1)
-        made = project(there, normed[0], wt_e, wp_e)
         att.qk(4)
-        mids = [end_mid(last, 0, res[0])]
-        att.soften(2)
+        att.mix(2)
+        stage(next0)
         att.norm(0)
-        att.mix(2)
-        stage(made)
+        att.soften(3)
         att.qk(5)
-        mids.append(end_mid(last, 1, res[1]))
-        hidden = [widen(mids[0])]
-        att.soften(3)
-        att.norm(1)
+        att.norm(2)
+        hidden0 = widen(mid0)
+        mid1 = end_mid(last, 1, res1)
+        att.soften(4)
+        att.qk(6)
         att.mix(3)
-        hidden.append(widen(mids[1]))
-        att.qk(6)
-        delta = [mids[0][0] + dot(hidden[0], w2_ref[...])]
-        att.soften(4)
-        att.norm(2)
+        delta0 = mid0[0] + dot(hidden0, w2_ref[...])
+        hidden1 = widen(mid1)
         att.gate(0)
+        att.qk(7)
+        next1 = project(there + 1, normed1, wt_e, wp_e)
+        delta1 = mid1[0] + dot(hidden1, w2_ref[...])
+        att.hand_on(6)
+        att.hand_on(7)
+        att.norm(3)
+        store_block(send_d, got_d, last, delta0, delta1, 0, rows)
+        att.soften(5)
         att.mix(4)
-        made = project(there + 1, normed[1], wt_e, wp_e)
-        att.qk(7)
-        delta.append(mids[1][0] + dot(hidden[1], w2_ref[...]))
-        att.soften(5)
-        att.norm(3)
         att.mix(5)
-        stage(made)
-        store_block(send_d, got_d, last, delta[0], delta[1], 0, rows)
-        att.hand_on(6)
+        att.norm(5)
+        stage(next1)
         att.norm(4)
-        att.hand_on(7)
-        att.norm(5)
         att.gate(1)
 
     send_delta(pairs - 2, 1)

time: 50.1 us -> 47.2 us (0.942)
  Pallas kernels: 48.6 us -> 45.7 us
    pallas_call x1, Pallas kernels: 48.6 us -> 45.7 us  [local_fn(): pl.pallas_call(functools.partial(kernel, 'sp', group, early), out_shape=j...]
where the time goes in v6:
time: 47.2 us; the launch traced here: 47.1 us
  Pallas kernels  45.7 us (97%)
  local copies, waits for them, and re-layouts  1.41 us (3%)
    pallas_call x1, Pallas kernels, local_fn(): pl.pallas_call(functools.partial(kernel, 'sp', group, early), out_shape=j...  45.7 us
    unnamed x1, local copies, waits for them, and re-layouts  1.41 us

profile of v6, /device:TPU:112, one launch (start us, length us, event | category | flops | bytes accessed | tf_op | source)
XLA Modules:
  0.0 47.1 jit_solution(13540193810369372248)
XLA Ops:
  0.0 45.7 %shard_map.91 = f32[24,192,128]{2,1,0:T(8,128)S(1)} custom-call(f32[24,192,128]{2,1,0:T(8,128)} %z_hbm.1, bf16[128,512]{1,0:T(8,128)(2,1)} %wp_s_hbm.1, bf16[4,128]{1,0:T(4,128)(2,1)} %wb_s_hbm.1, bf16[128,128]{1,0:T(8,128)(2,1)} %wo_s_hbm.1, bf16[128,512]{1,0:T(8,128)(2,1)} %wp_e_hbm.1, bf16[4,128]{1,0:T(4,128)(2,1)} %wb_e_hbm.1, ...), custom_call_target="tpu_custom_call" | custom-call | tf_op jit(solution)/shard_map/pallas_call | solution.py:591
  45.7 1.4 %copy.11 = f32[24,192,128]{2,1,0:T(8,128)} copy(f32[24,192,128]{2,1,0:T(8,128)S(1)} %shard_map.91) | data formatting | bytes 4718592

commit v7 on v6

--- a/solution.py
+++ b/solution.py
@@ -286,7 +286,14 @@
     def bias_of(phase, src):
         return jnp.concatenate([got_bias[phase, src, part].astype(F32) for part in range(chunks)], axis=0)
 
+    def open_scores():
+        att = Attention([0])
+        for unit in range(2):
+            att.qk(unit)
+        return att
+
     transpose_weights(wp_e, wt_e)
+    opening = open_scores()
     for src in peers:
         drain(got_bias.at[0, src], bias_recv_sem.at[0, src])
     low = low_half((HALF, LANES))
@@ -322,43 +329,36 @@
     def end_normed(pair, sub):
         return duplicate_tail(layer_norm(y_ref[2 * pair + sub].astype(BF16).astype(F32)))
 
-    def prime(slot):
-        att = Attention([slot])
-        for unit in range(2):
-            att.qk(unit)
-        for unit in range(2):
-            att.hand_on(unit)
-
-    prime(0)
+    for unit in range(2):
+        opening.hand_on(unit)
 
     @pl.loop(0, pairs)
     def _(pair):
         even = lax.rem(pair, 2) == 0
-        for part in range(chunks - 1):
-            @pl.when(pair == chunk // 2 * (part + 1) + 2)
-            def _():
+        @pl.when(pair == pairs - 2)
+        def _():
+            for part in range(chunks - 1):
                 publish_bias(1, part)
 
-        @pl.when(pair == 2)
-        def _():
-            send_h_view(WIDE, wide_view(0, 1))
-
-        @pl.when(jnp.logical_and(jnp.logical_and(pair > 2, pair < held + 2), even))
-        def _():
-            send_h_view(WIDE, wide_view(pair - 3, 2))
-
-        @pl.when(jnp.logical_and(pair > held + 2, even))
-        def _():
-            send_first(pair - 3, 2)
+        @pl.when(pair == held + 1)
+        def _():
+            send_h_view(WIDE, wide_view(0, held))
+
+        @pl.when(pair == pairs - 4)
+        def _():
+            send_first(held, pairs - 5 - held)
+
+        @pl.when(pair == pairs - 2)
+        def _():
+            send_first(pairs - 5, 2)
 
         @pl.when(pair == pairs - 1)
         def _():
             send_first(pairs - 3, 1)
 
-        for part in range(chunks - 1):
-            @pl.when(pair == chunk // 2 * (part + 1) + 2)
-            def _():
-                send_bias_part(1, part, 1, alike + [partner], 1)
+        @pl.when(pair == pairs - 2)
+        def _():
+            send_bias_part(1, 0, chunks - 1, alike + [partner], 1)
 
         last = jnp.maximum(pair - 1, 0)
         older = jnp.maximum(pair - 2, 0)
@@ -441,6 +441,7 @@
     for sub in range(2):
         stage(project(sub, duplicate_tail(layer_norm(column(sub))), wt_e, wp_e))
 
+    opening = open_scores()
     for src in [partner] + others:
         drain(got_bias.at[1, src, most], bias_recv_sem.at[1, src])
     for src in peers:
@@ -448,7 +449,8 @@
     for src in range(group):
         bias_t[rows * src:rows * src + rows] = bias_of(1, src) * (1 / SHRINK)
 
-    prime(0)
+    for unit in range(2):
+        opening.hand_on(unit)
 
     def end_mid(pair, sub, res):
         upd = merge_tail(res)

time: 47.2 us -> 46.9 us (level)
  Pallas kernels: 45.7 us -> 45.1 us
    pallas_call x1, Pallas kernels: 45.7 us -> 45.1 us  [local_fn(): pl.pallas_call(functools.partial(kernel, 'sp', group, early), out_shape=j...]
where the time goes in v7:
time: 46.9 us; the launch traced here: 46.6 us
  Pallas kernels  45.1 us (96%)
  local copies, waits for them, and re-layouts  1.41 us (3%)
    pallas_call x1, Pallas kernels, local_fn(): pl.pallas_call(functools.partial(kernel, 'sp', group, early), out_shape=j...  45.1 us
    unnamed x1, local copies, waits for them, and re-layouts  1.41 us

profile of v7, /device:TPU:112, one launch (start us, length us, event | category | flops | bytes accessed | tf_op | source)
XLA Modules:
  0.0 46.6 jit_solution(16290728574294089083)
XLA Ops:
  0.0 45.1 %shard_map.91 = f32[24,192,128]{2,1,0:T(8,128)S(1)} custom-call(f32[24,192,128]{2,1,0:T(8,128)} %z_hbm.1, bf16[128,512]{1,0:T(8,128)(2,1)} %wp_s_hbm.1, bf16[4,128]{1,0:T(4,128)(2,1)} %wb_s_hbm.1, bf16[128,128]{1,0:T(8,128)(2,1)} %wo_s_hbm.1, bf16[128,512]{1,0:T(8,128)(2,1)} %wp_e_hbm.1, bf16[4,128]{1,0:T(4,128)(2,1)} %wb_e_hbm.1, ...), custom_call_target="tpu_custom_call" | custom-call | tf_op jit(solution)/shard_map/pallas_call | solution.py:593
  45.2 1.4 %copy.11 = f32[24,192,128]{2,1,0:T(8,128)} copy(f32[24,192,128]{2,1,0:T(8,128)S(1)} %shard_map.91) | data formatting | bytes 4718592

commit v8 on v7

--- a/solution.py
+++ b/solution.py
@@ -95,7 +95,7 @@
     pairs = rows // 2
     chunk = 8
     chunks = rows // chunk
-    late = pairs - 3
+    late = pairs - 2
     groups = rows // early
     held = pairs - 9
     me = lax.axis_index(axis)
@@ -474,17 +474,9 @@
                 wait_h(LAST + idx)
                 spread(idx, 0, pairs)
 
-        @pl.when(pair == 2)
+        @pl.when(pair > 1)
         def _():
-            send_delta(0, 1)
-
-        @pl.when(jnp.logical_and(pair > 2, lax.rem(pair, 2) == 0))
-        def _():
-            send_delta(pair - 3, 2)
-
-        @pl.when(pair == pairs - 1)
-        def _():
-            send_delta(pairs - 3, 1)
+            send_delta(pair - 2, 1)
 
         last = jnp.maximum(pair - 1, 0)
         ahead = jnp.minimum(pair + 1, pairs - 1)

time: 46.9 us -> 46.7 us (level)
  no operation moved by 1% of the time
where the time goes in v8:
time: 46.7 us; the launch traced here: 46.6 us
  Pallas kernels  45.1 us (97%)
  local copies, waits for them, and re-layouts  1.41 us (3%)
    pallas_call x1, Pallas kernels, local_fn(): pl.pallas_call(functools.partial(kernel, 'sp', group, early), out_shape=j...  45.1 us
    unnamed x1, local copies, waits for them, and re-layouts  1.41 us

profile of v8, /device:TPU:112, one launch (start us, length us, event | category | flops | bytes accessed | tf_op | source)
XLA Modules:
  0.0 46.6 jit_solution(11127536425384055242)
XLA Ops:
  0.0 45.1 %shard_map.91 = f32[24,192,128]{2,1,0:T(8,128)S(1)} custom-call(f32[24,192,128]{2,1,0:T(8,128)} %z_hbm.1, bf16[128,512]{1,0:T(8,128)(2,1)} %wp_s_hbm.1, bf16[4,128]{1,0:T(4,128)(2,1)} %wb_s_hbm.1, bf16[128,128]{1,0:T(8,128)(2,1)} %wo_s_hbm.1, bf16[128,512]{1,0:T(8,128)(2,1)} %wp_e_hbm.1, bf16[4,128]{1,0:T(4,128)(2,1)} %wb_e_hbm.1, ...), custom_call_target="tpu_custom_call" | custom-call | tf_op jit(solution)/shard_map/pallas_call | solution.py:585
  45.2 1.4 %copy.11 = f32[24,192,128]{2,1,0:T(8,128)} copy(f32[24,192,128]{2,1,0:T(8,128)S(1)} %shard_map.91) | data formatting | bytes 4718592

commit v9 on v8

--- a/solution.py
+++ b/solution.py
@@ -549,8 +549,6 @@
                 y_ref[row, low_col:low_col + 2 * count] += flat[pl.ds(low_col * rows + row, 2 * count, stride=rows), :]
 
     finish(0, 0, late)
-    finish(1, late, pairs - late)
-
     for peer in alike + [partner]:
         drain(send_bias.at[1, most], bias_send_sem.at[1, peer])
     for src in alike:
@@ -560,6 +558,7 @@
         for sem, view in enumerate(whole_views):
             drain(view(send_h, peer), h_send_sem.at[sem, peer])
         drain(send_d.at[peer], d_send_sem.at[peer])
+    finish(1, late, pairs - late)
 
 
 def solution(mesh):

time: 46.7 us -> 46.6 us (level)
  no operation moved by 1% of the time
where the time goes in v9:
time: 46.6 us; the launch traced here: 46.5 us
  Pallas kernels  45.1 us (97%)
  local copies, waits for them, and re-layouts  1.41 us (3%)
    pallas_call x1, Pallas kernels, local_fn(): pl.pallas_call(functools.partial(kernel, 'sp', group, early), out_shape=j...  45.1 us
    unnamed x1, local copies, waits for them, and re-layouts  1.41 us

profile of v9, /device:TPU:112, one launch (start us, length us, event | category | flops | bytes accessed | tf_op | source)
XLA Modules:
  0.0 46.5 jit_solution(112181169180258405)
XLA Ops:
  0.0 45.1 %shard_map.91 = f32[24,192,128]{2,1,0:T(8,128)S(1)} custom-call(f32[24,192,128]{2,1,0:T(8,128)} %z_hbm.1, bf16[128,512]{1,0:T(8,128)(2,1)} %wp_s_hbm.1, bf16[4,128]{1,0:T(4,128)(2,1)} %wb_s_hbm.1, bf16[128,128]{1,0:T(8,128)(2,1)} %wo_s_hbm.1, bf16[128,512]{1,0:T(8,128)(2,1)} %wp_e_hbm.1, bf16[4,128]{1,0:T(4,128)(2,1)} %wb_e_hbm.1, ...), custom_call_target="tpu_custom_call" | custom-call | tf_op jit(solution)/shard_map/pallas_call | solution.py:584
  45.1 1.4 %copy.11 = f32[24,192,128]{2,1,0:T(8,128)} copy(f32[24,192,128]{2,1,0:T(8,128)S(1)} %shard_map.91) | data formatting | bytes 4718592
